TPU v7x, 256 devices: a whole 4x4x8 slice. The times are simulated.
256 devices in a mesh: freq: 16 (over y_lo, x, core), base: 16 (over y_hi, z).
Axes of the slice: x: 4, y: 4 (y_hi: 2, y_lo: 2; y = y_hi * 2 + y_lo), z: 8, core: 2. Of those that a mesh axis runs over, the one named last changes fastest.
Arguments:
- visibility: float32 [2, 32, 8192], P(None, 'freq', 'base'), may hold values from -6 to 6
- tile_of: int32 [32, 8192, 1], P('freq', 'base'), may hold values from 0 to 15; in each aligned block of 512 rows (0 to 511, 512 to 1023, ..., all dimensions but the last counted through in order) at most 64 rows name the same one
- u_within: int32 [32, 8192], P('freq', 'base'), may hold values from 0 to 63
- v_cell: int32 [32, 8192], P('freq', 'base'), may hold values from 0 to 1016
- kernel_index: int32 [2, 32, 8192], P(None, 'freq', 'base'), may hold values from 0 to 127
- kernel: float32 [128, 8], replicated, may hold values from 0.1 to 1
- live_count: int32 [32, 16], P('freq', 'base'), may hold values from 64 to 512, as said below
- bin_map: int32 [1024, 1024], P('base'), may hold values from 0 to 511, as said below
Outputs:
- power_map: float32 [1024, 1024], P('freq', 'base')
- spectrum: float32 [512], replicated
Inputs may be any that keep to these rules, and one draw needn't show every extreme that they name: `tile_of`: among the visibilities of one channel on one device, at most 64 name the same tile, and in some device's visibilities a tile is named by exactly 64. `live_count`: the first device along base holds 512 used slots in every channel; the used slots of a device are its first ones. `bin_map`: every bin number occurs.
All inputs are finite; a program needn't handle non-finite values.
Results may differ from a plain program's by a relative error of at most 0.0003.
Values sent between devices are 32-bit elements; how exact they have to be, the bound alone decides.
A program may use at most 128 MiB of HBM per device.

v0:
```python
import functools
import math

import jax
import jax.numpy as jnp
from jax import lax
from jax.sharding import Mesh
from jax.sharding import PartitionSpec as P

G = 1024
NBINS = 512
KW = 8
BASE = ("base_0", "base_1")
FREQ = ("freq_0", "freq_1", "freq_2")
FREQ_BASE = ("freq_0", "freq_1", "freq_2", "base_0", "base_1")


HIGHEST_PRECISION = lax.Precision.HIGHEST


def passed_along(x, axis, by):
    peers = lax.axis_size(axis)
    pairs = [(i, i + by) for i in range(peers) if 0 <= i + by < peers]
    return lax.ppermute(x, axis, pairs)


def cut_along(x, dim, peers):
    before, after = (x.shape[:dim], x.shape[dim + 1 :])
    return jnp.moveaxis(x.reshape(*before, peers, -1, *after), dim, 0)


def sum_at_owner(x, axis, dim):
    peers = lax.axis_size(axis)
    tiles = lax.all_to_all(cut_along(x, dim, peers), axis, 0, 0, tiled=True)
    return jnp.sum(tiles, axis=0)


def over_axes(x, axes):
    return functools.reduce(lax.psum, axes, x)


def look_up_taps(kernel_index, kernel):
    table_rows = kernel.shape[0]
    onehot = (kernel_index[..., None] == jnp.arange(table_rows, dtype=jnp.int32)).astype(
        jnp.float32
    )
    return jnp.einsum("acno,ot->actn", onehot, kernel, precision=HIGHEST_PRECISION)


def visibility_fields(
    visibility, tile_of, u_within, v_cell, kernel_index, kernel, live_count, tile_rows
):
    slots = u_within.shape[1]
    is_live = jnp.arange(slots, dtype=jnp.int32)[None, :] < live_count
    zeroed = jnp.zeros_like(visibility[0])
    real_part = jnp.where(is_live, visibility[0], zeroed)
    imag_part = jnp.where(is_live, visibility[1], zeroed)
    tile_index = tile_of[:, :, 0]
    u_cell = jnp.minimum(tile_index * tile_rows + u_within, G - KW)
    u_cell = u_cell - tile_index * tile_rows
    taps = look_up_taps(kernel_index, kernel)
    fields = jnp.concatenate(
        [
            real_part[:, None],
            imag_part[:, None],
            u_cell[:, None].astype(jnp.float32),
            v_cell[:, None].astype(jnp.float32),
            taps[0],
            taps[1],
        ],
        axis=1,
    )
    return (fields, is_live, tile_index)


def row_taps(fields, row_start, row_count):
    u_cell = fields[2].astype(jnp.int32)
    offset = row_start + jnp.arange(row_count, dtype=jnp.int32)[None, :] - u_cell[:, None]
    taps = jnp.zeros(offset.shape, jnp.float32)
    for tap_index in range(KW):
        taps = taps + jnp.where(offset == tap_index, fields[4 + tap_index][:, None], 0.0)
    return taps


def column_side(fields):
    v_start = fields[3].astype(jnp.int32)
    offset = jnp.arange(G, dtype=jnp.int32)[None, :] - v_start[:, None]
    taps = jnp.zeros(offset.shape, jnp.float32)
    for tap_index in range(KW):
        taps = taps + jnp.where(offset == tap_index, fields[4 + KW + tap_index][:, None], 0.0)
    return jnp.concatenate([fields[0][:, None] * taps, fields[1][:, None] * taps], axis=1)


def contract_slots(upper, lower):
    return lax.dot_general(upper, lower, (((0,), (0,)), ((), ())), precision=HIGHEST_PRECISION)


def grid_rows(fields, row_start, row_count):
    return contract_slots(row_taps(fields, row_start, row_count), column_side(fields))


def dft_matrix():
    positions = jnp.arange(G, dtype=jnp.int32)
    phase = positions[:, None] * positions[None, :] % G
    angle = phase.astype(jnp.float32) * (2.0 * math.pi / G)
    cosine = jnp.cos(angle)
    sine = jnp.sin(angle)
    return jnp.concatenate(
        [jnp.concatenate([cosine, -sine], axis=1), jnp.concatenate([sine, cosine], axis=1)], axis=0
    )


def row_transform(grid_tile, dft_table, tile_rows, channels_here):
    flat_rows = grid_tile.reshape(tile_rows * channels_here, 2 * G)
    halves = jnp.stack(
        [
            jnp.dot(flat_rows, dft_table[:, :G], precision=HIGHEST_PRECISION),
            jnp.dot(flat_rows, dft_table[:, G:], precision=HIGHEST_PRECISION),
        ]
    )
    return halves.reshape(2, tile_rows, channels_here, G)


def to_columns(columns, tile_rows, channels_here):
    return columns.reshape(2 * G, channels_here * tile_rows)


def histogram(stacked, bins):
    row_total = bins.shape[0]
    block_rows = min(64, row_total)
    block_count = row_total // block_rows
    columns = bins.shape[1]
    value_blocks = stacked.reshape(2, block_count, block_rows * columns).transpose(1, 0, 2)
    bin_blocks = bins.reshape(block_count, block_rows * columns)

    def add_block(running, pieces):
        values, bin_ids = pieces
        onehot = (bin_ids[:, None] == jnp.arange(NBINS, dtype=jnp.int32)[None, :]).astype(
            jnp.float32
        )
        return (running + jnp.dot(values, onehot, precision=HIGHEST_PRECISION), None)

    result, _ = lax.scan(add_block, jnp.zeros((2, NBINS), jnp.float32), (value_blocks, bin_blocks))
    return result


def per_device(visibility, tile_of, u_within, v_cell, kernel_index, kernel, live_count, bin_map):
    base_count = lax.axis_size(BASE)
    freq_count = lax.axis_size(FREQ)
    tile_rows = G // base_count
    channels_here = visibility.shape[1]
    slots = visibility.shape[2]
    dft_table = dft_matrix()
    fields, is_live, tile_index = visibility_fields(
        visibility, tile_of, u_within, v_cell, kernel_index, kernel, live_count, tile_rows
    )
    capacity = 2 * slots // base_count
    field_count = fields.shape[1]
    chosen = (
        (tile_index[:, :, None] == jnp.arange(base_count, dtype=jnp.int32)[None, None, :])
        & is_live[:, :, None]
    ).astype(jnp.int32)
    before_count = jnp.sum((jnp.cumsum(chosen, axis=1) - chosen) * chosen, axis=2)
    target = jnp.where(is_live, tile_index * capacity + before_count, base_count * capacity)
    outgoing = []
    for channel in range(channels_here):
        placed = (
            jnp.zeros((base_count * capacity, field_count), jnp.float32)
            .at[target[channel]]
            .set(fields[channel].T, mode="drop")
        )
        outgoing.append(placed.reshape(base_count, capacity, field_count).transpose(0, 2, 1))
    received = lax.all_to_all(
        jnp.stack(outgoing, axis=1), BASE, split_axis=0, concat_axis=0, tiled=True
    )
    extended = []
    for channel in range(channels_here):
        slot_fields = (
            received[:, channel].transpose(1, 0, 2).reshape(field_count, base_count * capacity)
        )
        extended.append(grid_rows(slot_fields, 0, tile_rows + KW).reshape(tile_rows + KW, 2, G))
    extended = jnp.stack(extended, axis=1)
    incoming = passed_along(extended[tile_rows:], BASE, 1)
    grid_tile = extended[:tile_rows].at[:KW].add(incoming)
    halves = row_transform(grid_tile, dft_table, tile_rows, channels_here)
    columns = lax.all_to_all(halves, BASE, split_axis=3, concat_axis=1, tiled=True)
    stacked = to_columns(columns, tile_rows, channels_here)
    spectra = contract_slots(dft_table, stacked)
    normalizer = 1.0 / (channels_here * freq_count * slots * base_count)
    squared = spectra[:G] * spectra[:G] + spectra[G:] * spectra[G:]
    power_part = jnp.sum(squared.reshape(G, channels_here, tile_rows), axis=1) * normalizer
    bins_here = bin_map.T
    share_rows = G // freq_count
    share_start = lax.axis_index(FREQ) * share_rows
    power_share = sum_at_owner(power_part, FREQ, 0)
    bins_share = lax.dynamic_slice_in_dim(bins_here, share_start, share_rows, 0)
    bin_sums_local = histogram(jnp.stack([power_share, jnp.ones_like(power_share)]), bins_share)
    totals, counts = (
        over_axes(bin_sums_local[0], FREQ_BASE),
        over_axes(bin_sums_local[1], FREQ_BASE),
    )
    return (power_share, totals / counts)


def solution(mesh):
    split = Mesh(
        mesh.devices.reshape(2, 4, 2, 2, 8), ("freq_0", "freq_1", "freq_2", "base_0", "base_1")
    )
    return jax.shard_map(
        per_device,
        mesh=split,
        in_specs=(
            P(None, FREQ, BASE),
            P(FREQ, BASE, None),
            P(FREQ, BASE),
            P(FREQ, BASE),
            P(None, FREQ, BASE),
            P(),
            P(FREQ, BASE),
            P(BASE, None),
        ),
        out_specs=(P(FREQ, BASE), P()),
        check_vma=False,
    )
```

profile of v0, /device:TPU:2, one launch (start us, length us, event | category | flops | bytes accessed | tf_op | source)
XLA Modules:
  0.0 249.1 jit_solution(13483670614798365430)
XLA Ops:
  3.5 2.3 reduce-window.6
  7.8 1.6 convolution_bitcast_fusion
  11.3 1.8 scatter_custom_fusion
  13.5 1.8 scatter_custom_fusion.1
  16.9 11.4 %all-to-all-start = ((f32[16,1,2560]{2,1,0:T(1,128)}), f32[16,1,2560]{2,1,0:T(1,128)S(1)}, u32[]{:S(2)}, u32[]{:S(2)}) async-start(f32[16,1,2560]{2,1,0:T(1,128)} %reshape.433), calls=%async_computation | async-start | bytes 327680 | tf_op jit(solution)/shard_map/all_to_all | solution.py:173
  28.3 17.5 %fusion.34 = (f32[1024,1024]{1,0:T(8,128)}, f32[1024,1024]{1,0:T(8,128)}) fusion(), kind=kLoop, calls=%fused_computation.52 | loop fusion | flops 14680064 | bytes 8388608 | tf_op jit(solution)/shard_map/sin | solution.py:107
  45.8 16.5 %fusion.36 = f32[1024,1024]{1,0:T(8,128)} fusion(), kind=kLoop, calls=%fused_computation.54 | loop fusion | flops 15728640 | bytes 4194304 | tf_op jit(solution)/shard_map/neg | solution.py:109
  65.9 3.9 %broadcast_multiply_fusion.1 = (f32[1024,1024]{1,0:T(8,128)S(1)}, f32[1024,1024]{1,0:T(8,128)S(1)}) fusion(f32[1024]{0:T(1024)S(1)} %mul.134, f32[1024]{0:T(1024)S(1)} %broadcast_in_dim.362, f32[1024]{0:T(1024)S(1)} %broadcast_in_dim.360, f32[1024]{0:T(1024)S(1)} %broadcast_in_dim.358, f32[1024]{0:T(1024)S(1)} %broadcast_in_dim.356, ...), kind=kLoop, calls=%fused_computation.49 | loop fusion | flops 27262976 | bytes 8433664 | tf_op jit(solution)/shard_map/mul | solution.py:91
  69.8 6.3 %fusion.6 = f32[72,2048]{1,0:T(8,128)S(1)} fusion(f32[1024,1024]{1,0:T(8,128)S(1)} %get-tuple-element.85, f32[1024,1024]{1,0:T(8,128)S(1)} %get-tuple-element.84, f32[1024]{0:T(1024)S(1)} %broadcast_in_dim.346, f32[1024]{0:T(1024)S(1)} %broadcast_in_dim.344, f32[1024]{0:T(1024)S(1)} %broadcast_in_dim.342, f32[1024]{0:T(1024)S(1)} %broadcast_in_dim.340, ...), kind=kOutput, calls=%fused_computation.11 | convolution fusion | flops 1815805952 | bytes 9015296 | tf_op jit(solution)/shard_map/dot_general | solution.py:95
  78.0 4.1 %broadcast_multiply_fusion.3 = (f32[1024,1024]{1,0:T(8,128)S(1)}, f32[1024,1024]{1,0:T(8,128)S(1)}) fusion(f32[1024]{0:T(1024)S(1)} %mul.127, f32[1024]{0:T(1024)S(1)} %broadcast_in_dim.330, f32[1024]{0:T(1024)S(1)} %broadcast_in_dim.328, f32[1024]{0:T(1024)S(1)} %broadcast_in_dim.326, f32[1024]{0:T(1024)S(1)} %broadcast_in_dim.324, ...), kind=kLoop, calls=%fused_computation.51 | loop fusion | flops 27262976 | bytes 8433664 | tf_op jit(solution)/shard_map/mul | solution.py:91
  82.1 6.4 %fusion.2 = f32[72,2048]{1,0:T(8,128)S(1)} fusion(f32[1024,1024]{1,0:T(8,128)S(1)} %get-tuple-element.87, f32[1024,1024]{1,0:T(8,128)S(1)} %get-tuple-element.86, f32[1024]{0:T(1024)S(1)} %broadcast_in_dim.313, f32[1024]{0:T(1024)S(1)} %broadcast_in_dim.311, f32[1024]{0:T(1024)S(1)} %broadcast_in_dim.309, f32[1024]{0:T(1024)S(1)} %broadcast_in_dim.307, ...), kind=kOutput, calls=%fused_computation.7 | convolution fusion | flops 1815805952 | bytes 9015296 | tf_op jit(solution)/shard_map/dot_general | solution.py:95
  89.2 3.9 %collective-permute-start = (f32[8,2,2,1024]{3,2,0,1:T(2,128)S(1)}, f32[8,2,2,1024]{3,2,0,1:T(2,128)S(1)}, u32[]{:S(2)}, u32[]{:S(2)}) collective-permute-start(f32[8,2,2,1024]{3,2,0,1:T(2,128)S(1)} %slice.365), channel_id=1, source_target_pairs={{0,1},{1,2},{2,3},{3,4},{4,5},{5,6},{6,7},{7,8},{8,9},{9,10},{10,1... | collective-permute-start | bytes 393224 | tf_op jit(solution)/shard_map/ppermute | solution.py:24
  93.1 16.1 %maximum_maximum_fusion = f32[2048,2048]{1,0:T(8,128)} fusion(f32[1024,1024]{1,0:T(8,128)} %get-tuple-element.101, f32[1024,1024]{1,0:T(8,128)} %get-tuple-element.100, f32[1024,1024]{1,0:T(8,128)} %fusion.36), kind=kLoop, calls=%fused_computation.2 | loop fusion | flops 12582912 | bytes 29360128 | tf_op jit(solution)/shard_map/concatenate | solution.py:108
  110.2 7.2 %fusion.37 = f32[1,64,2,1024]{3,1,2,0:T(8,128)S(1)} fusion(f32[64,2,2048]{2,0,1:T(8,128)S(1)} %reshape.406, f32[2048,2048]{1,0:T(8,128)} %maximum_maximum_fusion), kind=kOutput, calls=%fused_computation.55 | convolution fusion | flops 3221225472 | bytes 9961472 | tf_op jit(solution)/shard_map/dot_general | solution.py:117
  117.4 7.2 %fusion.38 = f32[1,64,2,1024]{3,1,2,0:T(8,128)S(1)} fusion(f32[64,2,2048]{2,0,1:T(8,128)S(1)} %reshape.406, f32[2048,2048]{1,0:T(8,128)} %maximum_maximum_fusion), kind=kOutput, calls=%fused_computation.56 | convolution fusion | flops 3221225472 | bytes 9961472 | tf_op jit(solution)/shard_map/dot_general | solution.py:118
  124.8 1.4 copy.56
  126.2 2.2 reshape.435
  128.4 35.2 %all_to_all.25 = f32[16,1,16384]{2,1,0:T(1,128)S(1)} all-to-all(f32[16,1,16384]{2,1,0:T(1,128)S(1)} %reshape.435), channel_id=1, replica_groups=mesh['freq_0'=2,'freq_1'=4,'freq_2'=2,'base_0'=2,'base_1'=8] {'base_0','..., dimensions={0} | all-to-all | bytes 2097152 | tf_op jit(solution)/shard_map/all_to_all | solution.py:186
  163.6 3.1 %reduce.5 = f32[16,16384]{1,0:T(8,128)S(1)} reduce(f32[16,1,16384]{2,1,0:T(1,128)S(1)} %all_to_all.25, f32[]{:T(128)} %broadcast.411), dimensions={1}, to_apply=%all_to_all.18.reduce_sub_computation | reduce | bytes 2097156 | tf_op jit(solution)/shard_map/all_to_all | solution.py:186
  166.8 1.5 reshape.436
  168.3 2.6 %copy.89 = f32[2,64,2,16,64]{1,3,0,4,2:T(8,128)} copy(f32[2,64,2,16,64]{1,2,0,4,3:T(2,128)S(1)} %bitcast.129) | data formatting | bytes 2097152 | tf_op jit(solution)/shard_map/all_to_all | solution.py:186
  170.9 2.1 reshape.407
  173.0 16.9 %fusion.171 = f32[2048,128]{0,1:T(8,128)S(1)} fusion(f32[2048,128]{0,1:T(8,128)S(1)} %reshape.407, f32[1024,1024]{1,0:T(8,128)} %get-tuple-element.101, f32[1024,1024]{1,0:T(8,128)} %get-tuple-element.100, f32[1024,1024]{1,0:T(8,128)} %fusion.36), kind=kOutput, calls=%fused_computation.215 | convolution fusion | flops 6455033856 | bytes 14680064 | tf_op jit(solution)/shard_map/dot_general | solution.py:95
  191.3 5.3 %all-to-all-start.2 = ((f32[16,1,4096]{2,1,0:T(1,128)}), f32[16,1,4096]{2,1,0:T(1,128)S(1)}, u32[]{:S(2)}, u32[]{:S(2)}) async-start(f32[16,1,4096]{2,1,0:T(1,128)} %reshape.437), calls=%async_computation.2 | async-start | bytes 524288 | tf_op jit(solution)/shard_map/all_to_all | solution.py:34
  196.9 5.0 %all-to-all-done.2 = f32[16,1,4096]{2,1,0:T(1,128)S(1)} async-done(((f32[16,1,4096]{2,1,0:T(1,128)}), f32[16,1,4096]{2,1,0:T(1,128)S(1)}, u32[]{:S(2)}, u32[]{:S(2)}) %all-to-all-start.2) | async-done | bytes 262176 | tf_op jit(solution)/shard_map/all_to_all | solution.py:34
  201.9 1.3 reduce.6
  204.3 2.7 %fusion.10 = f32[2,512]{1,0:T(2,128)S(1)} fusion(f32[2,4096]{1,0:T(2,128)S(1)} %squeeze.62, s32[4096]{0:T(1024)S(1)} %eq.198), kind=kOutput, calls=%fused_computation.16 | convolution fusion | flops 52428800 | bytes 53248 | tf_op jit(solution)/shard_map/while/body/eval_jaxpr/dot_general | solution.py:141
  207.0 4.9 %all-reduce.5 = (f32[512]{0:T(512)S(1)}, f32[512]{0:T(512)S(1)}) all-reduce(f32[512]{0:T(512)S(1)} %bitcast.143, f32[512]{0:T(512)S(1)} %bitcast.142), channel_id=1, replica_groups=mesh['freq_0'=2,'freq_1'=4,'freq_2'=2,'base_0'=2,'base_1'=8] {'freq_0'}, use_global_device_ids=true, to_apply=%region_7.8 | all-reduce | flops 1024 | bytes 8192 | tf_op jit(solution)/shard_map/psum | solution.py:39
  211.9 10.3 %all-reduce.2 = (f32[512]{0:T(512)S(1)}, f32[512]{0:T(512)S(1)}) all-reduce(f32[512]{0:T(512)S(1)} %get-tuple-element.38, f32[512]{0:T(512)S(1)} %get-tuple-element.39), channel_id=1, replica_groups=mesh['freq_0'=2,'freq_1'=4,'freq_2'=2,'base_0'=2,'base_1'=8] {'freq_1'}, use_global_device_ids=true, to_apply=%region_8.9 | all-reduce | flops 1024 | bytes 8192 | tf_op jit(solution)/shard_map/psum | solution.py:39
  222.2 2.5 all-reduce.4
  224.7 6.4 %all-reduce.3 = (f32[512]{0:T(512)S(1)}, f32[512]{0:T(512)S(1)}) all-reduce(f32[512]{0:T(512)S(1)} %get-tuple-element.36, f32[512]{0:T(512)S(1)} %get-tuple-element.37), channel_id=1, replica_groups=mesh['freq_0'=2,'freq_1'=4,'freq_2'=2,'base_0'=2,'base_1'=8] {'base_0'}, use_global_device_ids=true, to_apply=%region_10.11 | all-reduce | flops 1024 | bytes 8192 | tf_op jit(solution)/shard_map/psum | solution.py:39
  231.1 17.2 %all-reduce.1 = (f32[512]{0:T(512)S(1)}, f32[512]{0:T(512)S(1)}) all-reduce(f32[512]{0:T(512)S(1)} %get-tuple-element.34, f32[512]{0:T(512)S(1)} %get-tuple-element.35), channel_id=1, replica_groups=mesh['freq_0'=2,'freq_1'=4,'freq_2'=2,'base_0'=2,'base_1'=8] {'base_1'}, use_global_device_ids=true, to_apply=%region_11.12 | all-reduce | flops 1024 | bytes 8192 | tf_op jit(solution)/shard_map/psum | solution.py:39
  (105 shorter events, 19.1 us)
Async XLA Ops:
  0.6 196.0 %copy-start = (s32[64,1024]{1,0:T(8,128)S(1)}, s32[64,1024]{1,0:T(8,128)}, u32[]{:S(2)}) copy-start(s32[64,1024]{1,0:T(8,128)} %param.17) | copy-start | bytes 786436
  16.9 45.4 %all-to-all-start = ((f32[16,1,2560]{2,1,0:T(1,128)}), f32[16,1,2560]{2,1,0:T(1,128)S(1)}, u32[]{:S(2)}, u32[]{:S(2)}) async-start(f32[16,1,2560]{2,1,0:T(1,128)} %reshape.433), calls=%async_computation | async-start | bytes 327680 | tf_op jit(solution)/shard_map/all_to_all | solution.py:173
  89.2 20.1 %collective-permute-start = (f32[8,2,2,1024]{3,2,0,1:T(2,128)S(1)}, f32[8,2,2,1024]{3,2,0,1:T(2,128)S(1)}, u32[]{:S(2)}, u32[]{:S(2)}) collective-permute-start(f32[8,2,2,1024]{3,2,0,1:T(2,128)S(1)} %slice.365), channel_id=1, source_target_pairs={{0,1},{1,2},{2,3},{3,4},{4,5},{5,6},{6,7},{7,8},{8,9},{9,10},{10,1... | collective-permute-start | bytes 393224 | tf_op jit(solution)/shard_map/ppermute | solution.py:24
  191.3 10.5 %all-to-all-start.2 = ((f32[16,1,4096]{2,1,0:T(1,128)}), f32[16,1,4096]{2,1,0:T(1,128)S(1)}, u32[]{:S(2)}, u32[]{:S(2)}) async-start(f32[16,1,4096]{2,1,0:T(1,128)} %reshape.437), calls=%async_computation.2 | async-start | bytes 524288 | tf_op jit(solution)/shard_map/all_to_all | solution.py:34
where the time goes:
time: 254 us; the launch traced here: 249 us
  blocking collectives  76.5 us (30%)
  other arithmetic  71.4 us (28%)
  matrix products  48.3 us (19%)
  local copies, waits for them, and re-layouts  26 us (10%)
  starting transfers between devices  20.6 us (8%)
  waiting for transfers between devices  5.01 us (2%)
    psum x5, blocking collectives, over_axes(): return functools.reduce(lax.psum, axes, x)  41.3 us
    all_to_all x1, blocking collectives, per_device(): lax.all_to_all(halves, BASE, split_axis=3, concat_axis=1, tiled=True)  35.2 us
    dot_general x3, matrix products, contract_slots(): lax.dot_general(upper, lower, (((0,), (0,)), ((), ())), precision=HIGHEST...  29.6 us
    sin x1, other arithmetic, dft_matrix(): sine = jnp.sin(angle)  17.5 us
    neg x1, other arithmetic, dft_matrix(): -sine  16.5 us
    concatenate x1, other arithmetic, dft_matrix(): jnp.concatenate([jnp.concatenate([cosine, -sine], axis=1), jnp.concatenat...  16.1 us
    all_to_all x1, starting transfers between devices, per_device(): lax.all_to_all(jnp.stack(outgoing, axis=1), BASE, split_axis=0, concat_ax...  11.4 us
    mul x2, other arithmetic, column_side(): fields[0][:, None] * taps  8.02 us
  transfers between devices with their start and end apart: 3, of which 1 were waited for; matrix products, arithmetic and copies ran while one was open for 20% of the time, Pallas kernels for 0%

commit v1 on v0

v1 whole, which is shorter than its diff:
```python
import functools
import math

import jax
import jax.numpy as jnp
from jax import lax
from jax.experimental import pallas as pl
from jax.experimental.pallas import tpu as pltpu
from jax.sharding import Mesh
from jax.sharding import PartitionSpec as P

G = 1024
NBINS = 512
KW = 8
OVER = 128
SLOTS = 512
TILES = 16
BLOCKS = 128
F32 = jnp.float32
BF16 = jnp.bfloat16
I32 = jnp.int32
AXES = ("freq_0", "freq_1", "freq_2", "base_0", "base_1")
FREQ = AXES[:3]
BASE = AXES[3:]
NORM = 1.0 / (32 * 8192)


def iota(shape, dim):
    return lax.broadcasted_iota(I32, shape, dim)


def cis(phase, period):
    phase = phase & (period - 1)
    phase = jnp.where(phase >= period // 2, phase - period, phase)
    angle = phase.astype(F32) * (2.0 * math.pi / period)
    return jnp.cos(angle), -jnp.sin(angle)


def cmul(ar, ai, br, bi):
    return ar * br - ai * bi, ar * bi + ai * br


def split2(x):
    hi = x.astype(BF16)
    return hi, (x - hi.astype(F32)).astype(BF16)


def dot_nt(a, b):
    return lax.dot_general(a, b, (((1,), (1,)), ((), ())), preferred_element_type=F32)


def dot_nn(a, b):
    return lax.dot_general(a, b, (((1,), (0,)), ((), ())), preferred_element_type=F32)


def take_lanes(table, index):
    return jnp.take_along_axis(table, index, axis=1, mode="promise_in_bounds")


def bin_channel(ch, z, vis_ref, tile_ref, within_ref, vcell_ref, kidx_ref, live, upper):
    tile = tile_ref[ch : ch + 1, :]
    lane = iota((1, SLOTS), 1)
    is_live = lane < live
    member = (tile == iota((TILES, SLOTS), 0)) & is_live
    before = dot_nn(member.astype(BF16), upper)
    rank = jnp.sum(jnp.where(member, before, 0.0), axis=0, keepdims=True).astype(I32)
    block = tile * 4 + (rank >> 4)
    position = (block >> 3) * 128 + (((block & 7) + z) & 7) * 16 + (rank & 15)
    position = jnp.where(is_live, position, -1)
    row = jnp.minimum(within_ref[ch : ch + 1, :], (G - KW) - tile * 64)
    column = vcell_ref[ch : ch + 1, :]
    parts = []
    for part in range(2):
        value = vis_ref[part, ch : ch + 1, :]
        for _ in range(3):
            piece = value.astype(BF16).astype(F32)
            parts.append(piece)
            value = value - piece
    parts += [
        row.astype(F32),
        (column >> 3).astype(F32),
        (column & 7).astype(F32),
        kidx_ref[0, ch : ch + 1, :].astype(F32),
        kidx_ref[1, ch : ch + 1, :].astype(F32),
        jnp.ones((1, SLOTS), F32),
        jnp.zeros((4, SLOTS), F32),
    ]
    payload = jnp.concatenate(parts, axis=0).astype(BF16)
    out = []
    for part in range(4):
        place = (iota((256, SLOTS), 0) + part * 256 == position).astype(F32).astype(BF16)
        got = dot_nt(payload, place)
        out.append(
            jnp.concatenate(
                [
                    got[0:1] + got[1:2] + got[2:3],
                    got[3:4] + got[4:5] + got[5:6],
                    got[6:7],
                    got[7:8] * 8.0 + got[8:9],
                    got[9:10],
                    got[10:11],
                    got[11:12],
                    jnp.zeros((1, 256), F32),
                ],
                axis=0,
            )
        )
    return out


def bin_kernel(live_ref, vis_ref, tile_ref, within_ref, vcell_ref, kidx_ref, out_ref):
    z = lax.axis_index("base_1")
    upper = (iota((SLOTS, SLOTS), 0) < iota((SLOTS, SLOTS), 1)).astype(F32).astype(BF16)
    for ch in range(2):
        parts = bin_channel(
            ch, z, vis_ref, tile_ref, within_ref, vcell_ref, kidx_ref, live_ref[ch, 0], upper
        )
        for index, part in enumerate(parts):
            out_ref[ch, 2 * index] = part[:, :128]
            out_ref[ch, 2 * index + 1] = part[:, 128:]


def image_kernel(
    got_ref,
    kernel_ref,
    out_ref,
    merged,
    ec_ref,
    es_ref,
    pc_ref,
    ps_ref,
    wh_a,
    wl_a,
    rh_a,
    rl_a,
    wh_b,
    wl_b,
    rh_b,
    rl_b,
    grid_ref,
    bh_ref,
    bl_ref,
    mh_ref,
    ml_ref,
    tw_ref,
    count_vmem,
    count_smem,
    order,
    sem,
):
    z = lax.axis_index("base_1")
    group = iota((8, 128), 1) >> 4
    for half in range(2):
        for g in range(8):
            rows = [got_ref[zz, half, g] for zz in range(8)]
            for i in range(8):
                block = rows[(0 - i) % 8]
                for p in range(1, 8):
                    block = jnp.where(group == p, rows[(p - i) % 8], block)
                merged[half * 64 + g * 8 + i] = block
    merged[BLOCKS] = jnp.zeros((8, 128), F32)
    used = merged[0:BLOCKS, 6, :].astype(BF16)
    counts = dot_nt(jnp.ones((8, 128), F32).astype(BF16), used)
    count_vmem[...] = counts.astype(I32)
    copy = pltpu.make_async_copy(count_vmem, count_smem, sem)
    copy.start()

    l_row = iota((128, 128), 0)
    l_val = (l_row & 63) + (l_row >> 6) * 512 + z * 64
    lane = iota((128, 128), 1)
    ec, es = cis(l_val * lane, G)
    ec_ref[...] = ec
    es_ref[...] = es
    zr, zi = cis(l_val, G)
    kern = kernel_ref[...]
    pr = jnp.broadcast_to(kern[7:8], (128, 128))
    pi = jnp.zeros((128, 128), F32)
    for s in range(6, -1, -1):
        pr, pi = cmul(pr, pi, zr, zi)
        pr = pr + kern[s : s + 1]
    pc_ref[...] = pr
    ps_ref[...] = pi
    fc, fs = cis(l_row * lane, 128)
    for quarter, value in ((0, fc), (1, -fs), (2, fs), (3, fc)):
        hi, lo = split2(value)
        at = (slice((quarter >> 1) * 128, (quarter >> 1) * 128 + 128), slice((quarter & 1) * 128, (quarter & 1) * 128 + 128))
        mh_ref[at] = hi
        ml_ref[at] = lo
    tr, ti = cis(l_row, G)
    ar, ai = tr, ti
    for k0 in range(1, 8):
        tw_ref[k0, 0] = ar
        tw_ref[k0, 1] = ai
        if k0 < 7:
            ar, ai = cmul(ar, ai, tr, ti)
    sub = iota((8, 128), 0)
    ct_r, ct_i = cis(sub * iota((8, 128), 1), 8)
    grid_ref[...] = jnp.zeros_like(grid_ref)
    for ref in (wh_b, wl_b, rh_b, rl_b):
        ref[...] = jnp.zeros_like(ref)

    copy.wait()

    def list_step(b, n):
        order[n] = b
        return n + jnp.where(count_smem[0, b] > 0, 1, 0)

    total = lax.fori_loop(0, BLOCKS, list_step, 0, unroll=8)
    order[total] = BLOCKS
    order[total + 1] = BLOCKS

    def build(bid, wh, wl, rh, rl):
        blk = merged[bid]
        ints = blk.astype(I32)

        def spread(row):
            return jnp.broadcast_to(row, (8, 128))

        v = spread(ints[3:4])
        index_d = v & 127
        index_c = v >> 7
        index_u = spread(ints[4:5])
        index_v = spread(ints[5:6])
        w = spread(ints[2:3])
        cr = take_lanes(ct_r, index_c)
        ci = take_lanes(ct_i, index_c)
        cr, ci = cmul(cr, ci, spread(blk[0:1]), spread(blk[1:2]))
        for pair in range(8):
            res, ims = [], []
            for lg in (2 * pair, 2 * pair + 1):
                at = slice(8 * lg, 8 * lg + 8)
                er = take_lanes(ec_ref[at], index_d)
                ei = take_lanes(es_ref[at], index_d)
                qr = take_lanes(pc_ref[at], index_v)
                qi = take_lanes(ps_ref[at], index_v)
                ar, ai = cmul(er, ei, qr, qi)
                ar, ai = cmul(ar, ai, cr, ci)
                res.append(ar)
                ims.append(ai)
            for base, values in ((0, res), (128, ims)):
                hi, lo = split2(jnp.concatenate(values, axis=0))
                at = slice(base + 16 * pair, base + 16 * pair + 16)
                wh[at] = hi
                wl[at] = lo
        taps = take_lanes(kernel_ref[...], index_u)
        turned = jnp.take_along_axis(taps, (sub - w) & 7, axis=0, mode="promise_in_bounds")
        high = turned.astype(BF16).astype(F32)
        low = turned - high
        which = (w - sub + 7) >> 3
        zero = jnp.zeros((8, 128), F32)
        for pair in range(5):
            his, los = [], []
            for k in (2 * pair, 2 * pair + 1):
                hit = which == k
                his.append(jnp.where(hit, high, zero))
                los.append(jnp.where(hit, low, zero))
            rh[16 * pair : 16 * pair + 16] = jnp.concatenate(his, axis=0).astype(BF16)
            rl[16 * pair : 16 * pair + 16] = jnp.concatenate(los, axis=0).astype(BF16)

    def place(bid, wh, wl, rh, rl):
        res = dot_nt(rh[...], wh[...]) + dot_nt(rh[...], wl[...]) + dot_nt(rl[...], wh[...])
        start = pl.multiple_of(((bid >> 2) & 15) * 64, 64)
        grid_ref[pl.ds(start, 80), :] += res

    def step(pair, previous):
        first, second = order[2 * pair], order[2 * pair + 1]
        place(previous, wh_b, wl_b, rh_b, rl_b)
        build(first, wh_a, wl_a, rh_a, rl_a)
        place(first, wh_a, wl_a, rh_a, rl_a)
        build(second, wh_b, wl_b, rh_b, rl_b)
        return second

    last = lax.fori_loop(0, (total + 1) >> 1, step, jnp.int32(BLOCKS))
    place(last, wh_b, wl_b, rh_b, rl_b)

    root = math.sqrt(0.5)
    slot_of = (0, 2, 4, 6, 1, 3, 5, 7)
    for rows in range(8):
        u = [
            (
                grid_ref[128 * a + 16 * rows : 128 * a + 16 * rows + 16, 0:128],
                grid_ref[128 * a + 16 * rows : 128 * a + 16 * rows + 16, 128:256],
            )
            for a in range(8)
        ]

        def add(x, y):
            return x[0] + y[0], x[1] + y[1]

        def sub2(x, y):
            return x[0] - y[0], x[1] - y[1]

        def four(a, b, c, d):
            s, t = add(a, c), sub2(a, c)
            p, q = add(b, d), sub2(b, d)
            mq = (q[1], -q[0])
            return add(s, p), add(t, mq), sub2(s, p), sub2(t, mq)

        even = four(u[0], u[2], u[4], u[6])
        odd = four(u[1], u[3], u[5], u[7])
        o1 = ((odd[1][0] + odd[1][1]) * root, (odd[1][1] - odd[1][0]) * root)
        o2 = (odd[2][1], -odd[2][0])
        o3 = ((odd[3][1] - odd[3][0]) * root, -(odd[3][0] + odd[3][1]) * root)
        odd = (odd[0], o1, o2, o3)
        spectrum = [add(even[k], odd[k]) for k in range(4)] + [sub2(even[k], odd[k]) for k in range(4)]
        at = slice(16 * rows, 16 * rows + 16)
        for k0 in range(8):
            xr, xi = spectrum[k0]
            if k0:
                xr, xi = cmul(xr, xi, tw_ref[k0, 0, at], tw_ref[k0, 1, at])
            col = slice(128 * slot_of[k0], 128 * slot_of[k0] + 128)
            for base, value in ((0, xr), (128, xi)):
                hi, lo = split2(value)
                bh_ref[base + 16 * rows : base + 16 * rows + 16, col] = hi
                bl_ref[base + 16 * rows : base + 16 * rows + 16, col] = lo
    low_half = iota((128, 128), 1) < 64
    for k0 in range(4):
        col = slice(256 * k0, 256 * k0 + 256)
        full = dot_nn(mh_ref[...], bh_ref[:, col]) + dot_nn(mh_ref[...], bl_ref[:, col]) + dot_nn(ml_ref[...], bh_ref[:, col])
        power = (full[:128] * full[:128] + full[128:] * full[128:]) * NORM
        pa, pb = power[:, :128], power[:, 128:]
        ra, rb = pltpu.roll(pa, 64, 1), pltpu.roll(pb, 64, 1)
        out_ref[0, :, k0] = jnp.where(low_half, pa, rb).reshape(16, 8, 128)
        out_ref[1, :, k0] = jnp.where(low_half, ra, pb).reshape(16, 8, 128)


def image_call(got, kernel_t):
    w = pltpu.VMEM((256, 128), BF16)
    r = pltpu.VMEM((80, 128), BF16)
    t = pltpu.VMEM((128, 128), F32)
    return pl.pallas_call(
        image_kernel,
        out_shape=jax.ShapeDtypeStruct((2, 16, 4, 8, 128), F32),
        in_specs=[pl.BlockSpec(memory_space=pltpu.VMEM)] * 2,
        out_specs=pl.BlockSpec(memory_space=pltpu.VMEM),
        scratch_shapes=[
            pltpu.VMEM((BLOCKS + 1, 8, 128), F32),
            t, t, t, t,
            w, w, r, r, w, w, r, r,
            pltpu.VMEM((1040, 256), F32),
            pltpu.VMEM((256, 1024), BF16),
            pltpu.VMEM((256, 1024), BF16),
            pltpu.VMEM((256, 256), BF16),
            pltpu.VMEM((256, 256), BF16),
            pltpu.VMEM((8, 2, 128, 128), F32),
            pltpu.VMEM((8, 128), I32),
            pltpu.SMEM((8, 128), I32),
            pltpu.SMEM((BLOCKS + 2,), I32),
            pltpu.SemaphoreType.DMA,
        ],
    )(got, kernel_t)


def tail_kernel(got_ref, bins_ref, power_ref, sums_ref, onehot, left):
    total = got_ref[0]
    for index in range(1, 32):
        total = total + got_ref[index]
    for k0 in range(8):
        half = (k0 // 4) * 64
        power_ref[pl.ds(k0, 8, stride=8), :] = total[k0 % 4][:, half : half + 64]
    high_row = iota((4, 128), 0)
    for row in range(32):
        bins = bins_ref[row : row + 1, :]
        low = bins & 127
        at = slice(128 * row, 128 * row + 128)
        onehot[:, at] = (iota((128, 128), 0) == low).astype(F32).astype(BF16)
        hit = (bins >> 7) == high_row
        value = total[row // 8][row % 8 : row % 8 + 1]
        p0 = value.astype(BF16).astype(F32)
        p1 = (value - p0).astype(BF16).astype(F32)
        p2 = value - p0 - p1
        zero = jnp.zeros((4, 128), F32)
        pieces = [jnp.where(hit, p, zero) for p in (p0, p1, p2, jnp.ones((1, 128), F32))]
        left[:, at] = jnp.concatenate(pieces, axis=0).astype(BF16)
    got = dot_nt(left[...], onehot[...])
    sums_ref[0:4] = got[0:4] + got[4:8] + got[8:12]
    sums_ref[4:8] = got[12:16]


def tail_call(got, bins):
    return pl.pallas_call(
        tail_kernel,
        out_shape=(jax.ShapeDtypeStruct((64, 64), F32), jax.ShapeDtypeStruct((8, 128), F32)),
        in_specs=[pl.BlockSpec(memory_space=pltpu.VMEM)] * 2,
        out_specs=(pl.BlockSpec(memory_space=pltpu.VMEM),) * 2,
        scratch_shapes=[pltpu.VMEM((128, 4096), BF16), pltpu.VMEM((16, 4096), BF16)],
    )(got, bins)


def per_device(visibility, tile_of, u_within, v_cell, kernel_index, kernel, live_count, bin_map):
    vmem = pl.BlockSpec(memory_space=pltpu.VMEM)
    binned = pl.pallas_call(
        bin_kernel,
        out_shape=jax.ShapeDtypeStruct((2, 8, 8, 128), F32),
        in_specs=[pl.BlockSpec(memory_space=pltpu.SMEM)] + [vmem] * 5,
        out_specs=vmem,
    )(live_count, visibility, tile_of[:, :, 0], u_within, v_cell, kernel_index)
    mine = lax.all_to_all(binned, "base_0", 0, 0, tiled=True)
    got = lax.all_gather(mine, "base_1")
    power = image_call(got, kernel.T)
    pieces = power.reshape(32, 4, 8, 128)
    pieces = lax.all_to_all(pieces, ("base_0",) + FREQ, 0, 0, tiled=True)
    freq = lax.axis_index(FREQ)
    bins = lax.dynamic_slice_in_dim(bin_map, freq * 64, 64, 1)
    bins = bins.T.reshape(8, 2, 4, 64).transpose(2, 0, 1, 3).reshape(32, 128)
    share, sums = tail_call(pieces, bins)
    sums = lax.psum(sums, AXES)
    return share, (sums[:4] / sums[4:]).reshape(NBINS)


def solution(mesh):
    split = Mesh(mesh.devices.reshape(2, 4, 2, 2, 8), AXES)
    return jax.shard_map(
        per_device,
        mesh=split,
        in_specs=(
            P(None, FREQ, BASE),
            P(FREQ, BASE, None),
            P(FREQ, BASE),
            P(FREQ, BASE),
            P(None, FREQ, BASE),
            P(),
            P(FREQ, BASE),
            P(BASE, None),
        ),
        out_specs=(P(FREQ, BASE), P()),
        check_vma=False,
    )
```

time: 254 us -> 163 us (0.64)
  the two profiles are of different devices: /device:TPU:2 before, /device:TPU:1 now
where the time goes in v1:
time: 163 us; the launch traced here: 162 us
  blocking collectives  109 us (67%)
  Pallas kernels  24.3 us (15%)
  starting transfers between devices  12.8 us (8%)
  waiting for transfers between devices  10.5 us (6%)
  local copies, waits for them, and re-layouts  4.29 us (3%)
    psum x1, blocking collectives, per_device(): sums = lax.psum(sums, AXES)  74 us
    all_gather x1, blocking collectives, per_device(): got = lax.all_gather(mine, 'base_1')  25.3 us
    pallas_call x1, Pallas kernels, image_call(): pl.pallas_call(image_kernel, out_shape=jax.ShapeDtypeStruct((2, 16, 4, 8,...  19.5 us
    all_to_all x1, starting transfers between devices, per_device(): pieces = lax.all_to_all(pieces, ('base_0',) + FREQ, 0, 0, tiled=True)  12.8 us
    all_to_all x1, waiting for transfers between devices, per_device(): pieces = lax.all_to_all(pieces, ('base_0',) + FREQ, 0, 0, tiled=True)  10.5 us
    all_to_all x1, blocking collectives, per_device(): mine = lax.all_to_all(binned, 'base_0', 0, 0, tiled=True)  9.47 us
    unnamed x7, local copies, waits for them, and re-layouts  3.5 us
  transfers between devices with their start and end apart: 1, of which 1 were waited for; matrix products, arithmetic and copies ran while one was open for 1% of the time, Pallas kernels for 0%

profile of v1, /device:TPU:1, one launch (start us, length us, event | category | flops | bytes accessed | tf_op | source)
XLA Modules:
  0.0 162.0 jit_solution(13112783807333425063)
XLA Ops:
  0.6 0.0 copy-start
  0.6 1.3 copy.15.live_ref
  2.0 1.3 copy.21
  3.3 2.5 %shard_map.95 = f32[2,8,8,128]{3,2,1,0:T(8,128)} custom-call(s32[2,1]{1,0:T(2,128)} %copy.15.live_ref, f32[2,2,512]{2,1,0:T(2,128)} %vis_ref.1, s32[2,512]{1,0:T(2,128)} %bitcast.16, s32[2,512]{1,0:T(2,128)} %within_ref.1, s32[2,512]{1,0:T(2,128)} %vcell_ref.1, s32[2,2,512]{2,1,0:T(2,128)} %kidx_ref.1), custom_call_target="tpu_custom_call" | custom-call | tf_op jit(solution)/shard_map/pallas_call | solution.py:392
  5.8 9.5 %all_to_all.10 = f32[2,8,8,128]{3,2,1,0:T(8,128)S(1)} all-to-all(f32[2,8,8,128]{3,2,1,0:T(8,128)} %shard_map.95), channel_id=1, replica_groups=mesh['freq_0'=2,'freq_1'=4,'freq_2'=2,'base_0'=2,'base_1'=8] {'base_0'}, dimensions={0} | all-to-all | bytes 131072 | tf_op jit(solution)/shard_map/all_to_all | solution.py:398
  15.3 25.3 %all-gather = f32[16,8,8,128]{3,2,1,0:T(8,128)} all-gather(f32[2,8,8,128]{3,2,1,0:T(8,128)S(1)} %all_to_all.10), channel_id=2, replica_groups=mesh['freq_0'=2,'freq_1'=4,'freq_2'=2,'base_0'=2,'base_1'=8] {'base_1'}, dimensions={0}, use_global_device_ids=true | all-gather | bytes 589824 | tf_op jit(solution)/shard_map/all_gather | solution.py:399
  40.6 19.5 %shard_map.96 = f32[2,16,4,8,128]{4,3,2,1,0:T(8,128)} custom-call(f32[8,2,8,8,128]{4,3,2,1,0:T(8,128)} %bitcast.14, f32[8,128]{1,0:T(8,128)} %bitcast.17), custom_call_target="tpu_custom_call" | custom-call | tf_op jit(solution)/shard_map/pallas_call | solution.py:331
  60.1 12.8 %all-to-all-start.1 = ((f32[32,4,8,128]{3,2,1,0:T(8,128)}), f32[32,4,8,128]{3,2,1,0:T(8,128)S(1)}, u32[]{:S(2)}, u32[]{:S(2)}) async-start(f32[32,4,8,128]{3,2,1,0:T(8,128)} %bitcast.13), calls=%async_computation.1 | async-start | bytes 1048576 | tf_op jit(solution)/shard_map/all_to_all | solution.py:402
  72.9 0.0 copy-done
  72.9 0.1 constant_dynamic-slice_fusion
  73.0 0.1 copy.19
  73.1 0.7 reshape.18.bins_ref
  73.8 10.5 %all-to-all-done.1.got_ref = f32[32,4,8,128]{3,2,1,0:T(8,128)S(1)} async-done(((f32[32,4,8,128]{3,2,1,0:T(8,128)}), f32[32,4,8,128]{3,2,1,0:T(8,128)S(1)}, u32[]{:S(2)}, u32[]{:S(2)}) %all-to-all-start.1) | async-done | bytes 524320 | tf_op jit(solution)/shard_map/all_to_all | solution.py:402
  84.3 0.0 copy-start.1
  84.3 0.8 copy-done.1
  85.1 2.3 %shard_map.97 = (f32[64,64]{1,0:T(8,128)}, f32[8,128]{1,0:T(8,128)}) custom-call(f32[32,4,8,128]{3,2,1,0:T(8,128)} %copy-done.1, s32[32,128]{1,0:T(8,128)} %reshape.18.bins_ref), custom_call_target="tpu_custom_call" | custom-call | tf_op jit(solution)/shard_map/pallas_call | solution.py:381
  87.4 74.0 %psum.7 = f32[8,128]{1,0:T(8,128)S(1)} all-reduce(f32[8,128]{1,0:T(8,128)} %get-tuple-element.5), channel_id=1, replica_groups=mesh['freq_0'=2,'freq_1'=4,'freq_2'=2,'base_0'=2,'base_1'=8] {'freq_0','..., use_global_device_ids=true, to_apply=%region_0.0 | all-reduce | flops 1024 | bytes 8192 | tf_op jit(solution)/shard_map/psum | solution.py:407
  161.4 0.6 fusion
  (1 shorter events, 0.0 us)
Async XLA Ops:
  0.6 72.3 %copy-start = (s32[64,1024]{1,0:T(8,128)S(1)}, s32[64,1024]{1,0:T(8,128)}, u32[]{:S(2)}) copy-start(s32[64,1024]{1,0:T(8,128)} %param.15) | copy-start | bytes 786436
  60.1 24.2 %all-to-all-start.1 = ((f32[32,4,8,128]{3,2,1,0:T(8,128)}), f32[32,4,8,128]{3,2,1,0:T(8,128)S(1)}, u32[]{:S(2)}, u32[]{:S(2)}) async-start(f32[32,4,8,128]{3,2,1,0:T(8,128)} %bitcast.13), calls=%async_computation.1 | async-start | bytes 1048576 | tf_op jit(solution)/shard_map/all_to_all | solution.py:402
  84.3 0.8 copy-start.1

commit v2 on v1

v2 whole, which is shorter than its diff:
```python
import functools
import math

import jax
import jax.numpy as jnp
from jax import lax
from jax.experimental import pallas as pl
from jax.experimental.pallas import tpu as pltpu
from jax.sharding import PartitionSpec as P

G = 1024
NBINS = 512
KW = 8
OVER = 128
SLOTS = 512
TILES = 16
BLOCKS = 128
F32 = jnp.float32
BF16 = jnp.bfloat16
I32 = jnp.int32
MESH = pl.DeviceIdType.MESH
VMEM_SPEC = pl.BlockSpec(memory_space=pltpu.VMEM)
NORM = 1.0 / (32 * 8192)


def iota(shape, dim):
    return lax.broadcasted_iota(I32, shape, dim)


def cis(phase, period):
    phase = phase & (period - 1)
    phase = jnp.where(phase >= period // 2, phase - period, phase)
    angle = phase.astype(F32) * (2.0 * math.pi / period)
    return jnp.cos(angle), -jnp.sin(angle)


def cmul(ar, ai, br, bi):
    return ar * br - ai * bi, ar * bi + ai * br


def split2(x):
    hi = x.astype(BF16)
    return hi, (x - hi.astype(F32)).astype(BF16)


def dot_nt(a, b):
    return lax.dot_general(a, b, (((1,), (1,)), ((), ())), preferred_element_type=F32)


def dot_nn(a, b):
    return lax.dot_general(a, b, (((1,), (0,)), ((), ())), preferred_element_type=F32)


def take_lanes(table, index):
    return jnp.take_along_axis(table, index, axis=1, mode="promise_in_bounds")


def bin_channel(ch, z, vis_ref, tile_ref, within_ref, vcell_ref, kidx_ref, live, upper):
    tile = tile_ref[ch]
    lane = iota((1, SLOTS), 1)
    is_live = lane < live
    member = (tile == iota((TILES, SLOTS), 0)) & is_live
    before = dot_nn(member.astype(BF16), upper)
    rank = jnp.sum(jnp.where(member, before, 0.0), axis=0, keepdims=True).astype(I32)
    block = tile * 4 + (rank >> 4)
    position = (block >> 3) * 128 + (((block & 7) + z) & 7) * 16 + (rank & 15)
    position = jnp.where(is_live, position, -1)
    row = jnp.minimum(within_ref[ch : ch + 1, :], (G - KW) - tile * 64)
    column = vcell_ref[ch : ch + 1, :]
    parts = []
    for part in range(2):
        value = vis_ref[part, ch : ch + 1, :]
        for _ in range(3):
            piece = value.astype(BF16).astype(F32)
            parts.append(piece)
            value = value - piece
    parts += [
        row.astype(F32),
        (column >> 3).astype(F32),
        (column & 7).astype(F32),
        kidx_ref[0, ch : ch + 1, :].astype(F32),
        kidx_ref[1, ch : ch + 1, :].astype(F32),
        jnp.ones((1, SLOTS), F32),
        jnp.zeros((4, SLOTS), F32),
    ]
    payload = jnp.concatenate(parts, axis=0).astype(BF16)
    out = []
    for part in range(4):
        place = (iota((256, SLOTS), 0) + part * 256 == position).astype(F32).astype(BF16)
        got = dot_nt(payload, place)
        out.append(
            jnp.concatenate(
                [
                    got[0:1] + got[1:2] + got[2:3],
                    got[3:4] + got[4:5] + got[5:6],
                    got[6:7],
                    got[7:8] * 8.0 + got[8:9],
                    got[9:10],
                    got[10:11],
                    got[11:12],
                    jnp.zeros((1, 256), F32),
                ],
                axis=0,
            )
        )
    return out


def places():
    base = lax.axis_index("base")
    return base // 8, base % 8


def gather_kernel(
    live_ref, vis_ref, tile_ref, within_ref, vcell_ref, kidx_ref, out_ref, packed, got, send, land, relay, local
):
    h, z = places()
    hops = (1, -1, 2, -2)

    def device(side, step):
        return {"base": side * 8 + (z + step + 8) % 8}

    barrier = pltpu.get_barrier_semaphore()
    for step in hops:
        pl.semaphore_signal(barrier, 1, device_id=device(h, step), device_id_type=MESH)
    for step in (0,) + hops:
        pl.semaphore_signal(barrier, 1, device_id=device(1 - h, step), device_id_type=MESH)

    upper = (iota((SLOTS, SLOTS), 0) < iota((SLOTS, SLOTS), 1)).astype(F32).astype(BF16)
    for ch in range(2):
        parts = bin_channel(
            ch, z, vis_ref, tile_ref, within_ref, vcell_ref, kidx_ref, live_ref[0, ch], upper
        )
        for index, part in enumerate(parts):
            packed[ch, 12 * index : 12 * index + 6] = part[:6, :128]
            packed[ch, 12 * index + 6 : 12 * index + 12] = part[:6, 128:]
    pl.semaphore_wait(barrier, 9)

    def direct(side, step, number):
        return pltpu.make_async_remote_copy(
            src_ref=packed.at[side],
            dst_ref=got.at[z, h],
            send_sem=send.at[number],
            recv_sem=land.at[z, h],
            device_id=device(side, step),
            device_id_type=MESH,
        )

    def arrival(step, side):
        zz = (z + step + 8) % 8
        return pltpu.make_async_remote_copy(
            src_ref=got.at[zz, side],
            dst_ref=got.at[zz, side],
            send_sem=send.at[0],
            recv_sem=land.at[zz, side],
            device_id=device(1 - h, 0),
            device_id_type=MESH,
        )

    copies = []
    for step in (2, -2):
        copies.append(direct(1 - h, step, len(copies)))
        copies.append(direct(h, step, len(copies)))
    for step in (1, -1):
        copies.append(direct(1 - h, step, len(copies)))
        copies.append(direct(h, step, len(copies)))
    copies.append(direct(1 - h, 0, len(copies)))
    for copy in copies:
        copy.start()
    own = pltpu.make_async_copy(packed.at[h], got.at[z, h], local)
    own.start()

    relays = []

    def pass_on(source, side, step):
        zz = (z + source + 8) % 8
        copy = pltpu.make_async_remote_copy(
            src_ref=got.at[zz, side],
            dst_ref=got.at[zz, side],
            send_sem=relay.at[len(relays)],
            recv_sem=land.at[zz, side],
            device_id=device(h, step),
            device_id_type=MESH,
        )
        copy.start()
        relays.append(copy)

    arrival(-2, h).wait_recv()
    pass_on(-2, h, 2)
    pass_on(-2, h, 1)
    arrival(2, h).wait_recv()
    pass_on(2, h, -1)
    arrival(2, 1 - h).wait_recv()
    pass_on(2, 1 - h, -2)
    pass_on(2, 1 - h, -1)
    arrival(-2, 1 - h).wait_recv()
    pass_on(-2, 1 - h, 1)
    for step in (1, -1):
        arrival(step, h).wait_recv()
        arrival(step, 1 - h).wait_recv()
    arrival(0, 1 - h).wait_recv()
    for step in (3, -3, 4):
        arrival(step, h).wait_recv()
        arrival(step, 1 - h).wait_recv()
    own.wait()
    for copy in copies + relays:
        copy.wait_send()
    group = iota((48, 128), 1) >> 4
    for half in range(2):
        for i in range(8):
            block = got[(0 - i) % 8, half]
            for p in range(1, 8):
                block = jnp.where(group == p, got[(p - i) % 8, half], block)
            out_ref[half * 8 + i] = block


def gather_call(live, visibility, tile, within, column, kernel_index):
    return pl.pallas_call(
        gather_kernel,
        out_shape=jax.ShapeDtypeStruct((16, 48, 128), F32),
        in_specs=[pl.BlockSpec(memory_space=pltpu.SMEM)] + [VMEM_SPEC] * 5,
        out_specs=VMEM_SPEC,
        scratch_shapes=[
            pltpu.VMEM((2, 48, 128), F32),
            pltpu.VMEM((8, 2, 48, 128), F32),
            pltpu.SemaphoreType.DMA((9,)),
            pltpu.SemaphoreType.DMA((8, 2)),
            pltpu.SemaphoreType.DMA((6,)),
            pltpu.SemaphoreType.DMA,
        ],
        compiler_params=pltpu.CompilerParams(collective_id=0, has_side_effects=True),
    )(live, visibility, tile, within, column, kernel_index)


def grid_kernel(
    merged,
    kernel_ref,
    grid_ref,
    ec_ref,
    es_ref,
    pc_ref,
    ps_ref,
    wh_a,
    wl_a,
    rh_a,
    rl_a,
    wh_b,
    wl_b,
    rh_b,
    rl_b,
    count_vmem,
    count_smem,
    order,
    sem,
):
    _, z = places()
    used = (merged[...].reshape(768, 128) != 0.0).astype(F32).astype(BF16)
    counts = dot_nt(jnp.ones((8, 128), F32).astype(BF16), used)
    count_vmem[...] = counts.astype(I32)
    copy = pltpu.make_async_copy(count_vmem, count_smem, sem)
    copy.start()

    l_row = iota((128, 128), 0)
    l_val = (l_row & 63) + (l_row >> 6) * 512 + z * 64
    lane = iota((128, 128), 1)
    ec, es = cis(l_val * lane, G)
    ec_ref[...] = ec
    es_ref[...] = es
    zr, zi = cis(l_val, G)
    kern = kernel_ref[...]
    pr = jnp.broadcast_to(kern[7:8], (128, 128))
    pi = jnp.zeros((128, 128), F32)
    for s in range(6, -1, -1):
        pr, pi = cmul(pr, pi, zr, zi)
        pr = pr + kern[s : s + 1]
    pc_ref[...] = pr
    ps_ref[...] = pi
    sub = iota((8, 128), 0)
    ct_r, ct_i = cis(sub * iota((8, 128), 1), 8)
    grid_ref[...] = jnp.zeros_like(grid_ref)
    for ref in (wh_b, wl_b, rh_b, rl_b):
        ref[...] = jnp.zeros_like(ref)

    copy.wait()

    def list_step(b, n):
        order[n] = b
        first = ((b >> 6) * 8 + (b & 7)) * 48 + ((b >> 3) & 7) * 6
        found = count_smem[0, first] + count_smem[0, first + 1]
        return n + jnp.where(found > 0, 1, 0)

    total = lax.fori_loop(0, BLOCKS, list_step, 0, unroll=8)
    order[total] = BLOCKS
    order[total + 1] = BLOCKS

    def build(bid, wh, wl, rh, rl):
        which = ((bid >> 6) & 1) * 8 + (bid & 7)
        first = ((bid >> 3) & 7) * 6
        keep = jnp.where(bid < BLOCKS, 1.0, 0.0)

        def field(index):
            return jnp.broadcast_to(merged[which, pl.ds(first + index, 1), :], (8, 128))

        v = field(3).astype(I32)
        index_d = v & 127
        index_c = v >> 7
        index_u = field(4).astype(I32)
        index_v = field(5).astype(I32)
        w = field(2).astype(I32)
        cr = take_lanes(ct_r, index_c)
        ci = take_lanes(ct_i, index_c)
        cr, ci = cmul(cr, ci, field(0) * keep, field(1) * keep)
        for pair in range(8):
            res, ims = [], []
            for lg in (2 * pair, 2 * pair + 1):
                at = slice(8 * lg, 8 * lg + 8)
                er = take_lanes(ec_ref[at], index_d)
                ei = take_lanes(es_ref[at], index_d)
                qr = take_lanes(pc_ref[at], index_v)
                qi = take_lanes(ps_ref[at], index_v)
                ar, ai = cmul(er, ei, qr, qi)
                ar, ai = cmul(ar, ai, cr, ci)
                res.append(ar)
                ims.append(ai)
            for base, values in ((0, res), (128, ims)):
                hi, lo = split2(jnp.concatenate(values, axis=0))
                at = slice(base + 16 * pair, base + 16 * pair + 16)
                wh[at] = hi
                wl[at] = lo
        taps = take_lanes(kernel_ref[...], index_u)
        turned = jnp.take_along_axis(taps, (sub - w) & 7, axis=0, mode="promise_in_bounds")
        high = turned.astype(BF16).astype(F32)
        low = turned - high
        down = (w - sub + 7) >> 3
        zero = jnp.zeros((8, 128), F32)
        for pair in range(5):
            his, los = [], []
            for k in (2 * pair, 2 * pair + 1):
                hit = down == k
                his.append(jnp.where(hit, high, zero))
                los.append(jnp.where(hit, low, zero))
            rh[16 * pair : 16 * pair + 16] = jnp.concatenate(his, axis=0).astype(BF16)
            rl[16 * pair : 16 * pair + 16] = jnp.concatenate(los, axis=0).astype(BF16)

    def place(bid, wh, wl, rh, rl):
        res = dot_nt(rh[...], wh[...]) + dot_nt(rh[...], wl[...]) + dot_nt(rl[...], wh[...])
        start = pl.multiple_of(((bid >> 2) & 15) * 64, 64)
        grid_ref[pl.ds(start, 80), :] += res

    def step(pair, previous):
        first, second = order[2 * pair], order[2 * pair + 1]
        place(previous, wh_b, wl_b, rh_b, rl_b)
        build(first, wh_a, wl_a, rh_a, rl_a)
        place(first, wh_a, wl_a, rh_a, rl_a)
        build(second, wh_b, wl_b, rh_b, rl_b)
        return second

    last = lax.fori_loop(0, (total + 1) >> 1, step, jnp.int32(BLOCKS))
    place(last, wh_b, wl_b, rh_b, rl_b)

def grid_call(merged, kernel_t):
    w = pltpu.VMEM((256, 128), BF16)
    r = pltpu.VMEM((80, 128), BF16)
    t = pltpu.VMEM((128, 128), F32)
    return pl.pallas_call(
        grid_kernel,
        out_shape=jax.ShapeDtypeStruct((1040, 256), F32),
        in_specs=[VMEM_SPEC] * 2,
        out_specs=VMEM_SPEC,
        scratch_shapes=[
            t, t, t, t,
            w, w, r, r, w, w, r, r,
            pltpu.VMEM((8, 768), I32),
            pltpu.SMEM((8, 768), I32),
            pltpu.SMEM((BLOCKS + 2,), I32),
            pltpu.SemaphoreType.DMA,
        ],
    )(merged, kernel_t)


def tail_kernel(
    grid_ref, bins_ref, power_ref, spectrum_ref,
    bh_ref, bl_ref, mh_ref, ml_ref, tw_ref, turned, onehot, left,
    piece, partner, summed, landed, counts, counts_in, counts_z, counts_plane, totals, totals_in, totals_z, totals_plane,
    s_pair, r_pair, s_sum, r_sum, s_count, r_count, s_total, r_total, s_countz, r_countz, s_totalz, r_totalz,
):
    h, z = places()
    freq = lax.axis_index("freq")
    quad, core = freq // 2, freq % 2
    me = h * 16 + freq
    me_pair = h * 8 + quad

    def plane_device(index):
        return {"freq": index % 16, "base": (index // 16) * 8 + z}

    def column_device(index):
        return {"freq": freq, "base": h * 8 + index}

    barrier = pltpu.get_barrier_semaphore()

    def greet_plane(k, _):
        pl.semaphore_signal(barrier, 1, device_id=plane_device((me + k) % 32), device_id_type=MESH)
        return 0

    def greet_column(k, _):
        pl.semaphore_signal(barrier, 1, device_id=column_device((z + k) % 8), device_id_type=MESH)
        return 0

    lax.fori_loop(1, 32, greet_plane, 0)
    lax.fori_loop(1, 8, greet_column, 0)

    row128, lane128 = iota((128, 128), 0), iota((128, 128), 1)
    fc, fs = cis(row128 * lane128, 128)
    for quarter, value in ((0, fc), (1, -fs), (2, fs), (3, fc)):
        hi, lo = split2(value)
        at = (
            slice((quarter >> 1) * 128, (quarter >> 1) * 128 + 128),
            slice((quarter & 1) * 128, (quarter & 1) * 128 + 128),
        )
        mh_ref[at] = hi
        ml_ref[at] = lo
    tr, ti = cis(row128, G)
    ar, ai = tr, ti
    for k0 in range(1, 8):
        tw_ref[k0, 0] = ar
        tw_ref[k0, 1] = ai
        if k0 < 7:
            ar, ai = cmul(ar, ai, tr, ti)

    at = pl.multiple_of((freq // 2) * 128, 128)
    bins = bins_ref[:, pl.ds(at, 128)].astype(F32)
    bins = jnp.concatenate([bins, jnp.zeros((64, 128), F32)], axis=0)
    bins = pltpu.roll(bins, core * 64, 1)
    turned[...] = bins.T
    high_row = iota((4, 128), 0)
    lane8 = iota((8, 128), 1)
    hits = []
    for k0 in range(4):
        ours = turned[pl.ds(k0, 8, stride=8), :]
        other = turned[pl.ds(k0 + 4, 8, stride=8), :]
        both = jnp.where(lane8 < 64, ours, pltpu.roll(other, 64, 1)).astype(I32)
        for sub in range(8):
            row = 8 * k0 + sub
            found = both[sub : sub + 1]
            at = slice(128 * row, 128 * row + 128)
            onehot[:, at] = (row128 == (found & 127)).astype(F32).astype(BF16)
            hit = ((found >> 7) == high_row).astype(F32)
            left[12:16, at] = hit
            left[0:4, at] = hit
            left[4:8, at] = hit
            left[8:12, at] = hit
    got = dot_nt(left[...].astype(BF16), onehot[...])
    counts[...] = got[12:16]

    root = math.sqrt(0.5)
    slot_of = (0, 2, 4, 6, 1, 3, 5, 7)
    for rows in range(8):
        u = [
            (
                grid_ref[128 * a + 16 * rows : 128 * a + 16 * rows + 16, 0:128],
                grid_ref[128 * a + 16 * rows : 128 * a + 16 * rows + 16, 128:256],
            )
            for a in range(8)
        ]

        def add(x, y):
            return x[0] + y[0], x[1] + y[1]

        def sub2(x, y):
            return x[0] - y[0], x[1] - y[1]

        def four(a, b, c, d):
            s, t = add(a, c), sub2(a, c)
            p, q = add(b, d), sub2(b, d)
            mq = (q[1], -q[0])
            return add(s, p), add(t, mq), sub2(s, p), sub2(t, mq)

        even = four(u[0], u[2], u[4], u[6])
        odd = four(u[1], u[3], u[5], u[7])
        o1 = ((odd[1][0] + odd[1][1]) * root, (odd[1][1] - odd[1][0]) * root)
        o2 = (odd[2][1], -odd[2][0])
        o3 = ((odd[3][1] - odd[3][0]) * root, -(odd[3][0] + odd[3][1]) * root)
        odd = (odd[0], o1, o2, o3)
        spectrum = [add(even[k], odd[k]) for k in range(4)] + [sub2(even[k], odd[k]) for k in range(4)]
        at = slice(16 * rows, 16 * rows + 16)
        for k0 in range(8):
            xr, xi = spectrum[k0]
            if k0:
                xr, xi = cmul(xr, xi, tw_ref[k0, 0, at], tw_ref[k0, 1, at])
            col = slice(128 * slot_of[k0], 128 * slot_of[k0] + 128)
            for base, value in ((0, xr), (128, xi)):
                hi, lo = split2(value)
                bh_ref[base + 16 * rows : base + 16 * rows + 16, col] = hi
                bl_ref[base + 16 * rows : base + 16 * rows + 16, col] = lo
    pl.semaphore_wait(barrier, 38)

    def plane_copy(k, buf, slots, s, r):
        peer = (me + k) % 32
        return pltpu.make_async_remote_copy(
            src_ref=buf, dst_ref=slots.at[me], send_sem=s.at[k], recv_sem=r.at[me],
            device_id=plane_device(peer), device_id_type=MESH,
        )

    def column_copy(k, buf, slots, s, r):
        peer = (z + k) % 8
        return pltpu.make_async_remote_copy(
            src_ref=buf, dst_ref=slots.at[z], send_sem=s.at[k], recv_sem=r.at[z],
            device_id=column_device(peer), device_id_type=MESH,
        )

    def start_all(count, make, *args):
        def body(k, _):
            make(k, *args).start()
            return 0

        lax.fori_loop(1, count, body, 0)

    def wait_plane(buf, slots, s, r):
        def body(k, total):
            source = (me + k) % 32
            pltpu.make_async_remote_copy(
                src_ref=buf, dst_ref=slots.at[source], send_sem=s.at[k], recv_sem=r.at[source],
                device_id=plane_device(source), device_id_type=MESH,
            ).wait_recv()
            return total + slots[source]

        return lax.fori_loop(1, 32, body, buf[...])

    def wait_column(buf, slots, s, r):
        def body(k, total):
            source = (z + k) % 8
            pltpu.make_async_remote_copy(
                src_ref=buf, dst_ref=slots.at[source], send_sem=s.at[k], recv_sem=r.at[source],
                device_id=column_device(source), device_id_type=MESH,
            ).wait_recv()
            return total + slots[source]

        return lax.fori_loop(1, 8, body, buf[...])

    def sent_all(count, make, *args):
        def body(k, _):
            make(k, *args).wait_send()
            return 0

        lax.fori_loop(1, count, body, 0)

    plane_counts = (counts, counts_in, s_count, r_count)
    start_all(32, plane_copy, *plane_counts)

    def pair_copy(k0):
        return pltpu.make_async_remote_copy(
            src_ref=piece.at[1 - core, k0], dst_ref=partner.at[k0], send_sem=s_pair.at[k0], recv_sem=r_pair.at[k0],
            device_id={"freq": quad * 2 + 1 - core}, device_id_type=MESH,
        )

    low_half = iota((128, 128), 1) < 64
    for k0 in range(4):
        col = slice(256 * k0, 256 * k0 + 256)
        full = dot_nn(mh_ref[...], bh_ref[:, col]) + dot_nn(mh_ref[...], bl_ref[:, col]) + dot_nn(ml_ref[...], bh_ref[:, col])
        power = (full[:128] * full[:128] + full[128:] * full[128:]) * NORM
        pa, pb = power[:, :128], power[:, 128:]
        ra, rb = pltpu.roll(pa, 64, 1), pltpu.roll(pb, 64, 1)
        for side, block in ((0, jnp.where(low_half, pa, rb)), (1, jnp.where(low_half, ra, pb))):
            block = block.reshape(8, 2, 8, 128)
            for cc in range(2):
                piece[cc, k0, side] = block[:, cc]
        pair_copy(k0).start()
    for k0 in range(4):
        pair_copy(k0).wait_recv()
        for side in range(2):
            for q in range(8):
                summed[side * 8 + q, k0] = piece[core, k0, side, q] + partner[k0, side, q]

    def sum_copy(k):
        peer = (me_pair + k) % 16
        return pltpu.make_async_remote_copy(
            src_ref=summed.at[peer], dst_ref=landed.at[me_pair], send_sem=s_sum.at[k], recv_sem=r_sum.at[me_pair],
            device_id={"freq": (peer % 8) * 2 + core, "base": (peer // 8) * 8 + z}, device_id_type=MESH,
        )

    start_all(16, sum_copy)
    counts_plane[...] = wait_plane(*plane_counts)
    column_counts = (counts_plane, counts_z, s_countz, r_countz)
    start_all(8, column_copy, *column_counts)

    def wait_sum(k, total):
        source = (me_pair + k) % 16
        pltpu.make_async_remote_copy(
            src_ref=summed.at[source], dst_ref=landed.at[source], send_sem=s_sum.at[k], recv_sem=r_sum.at[source],
            device_id={"freq": (source % 8) * 2 + core, "base": (source // 8) * 8 + z}, device_id_type=MESH,
        ).wait_recv()
        return total + landed[source]

    total = lax.fori_loop(1, 16, wait_sum, summed[me_pair])
    for k0 in range(4):
        for sub in range(8):
            at = slice(128 * (8 * k0 + sub), 128 * (8 * k0 + sub) + 128)
            hit = left[12:16, at]
            value = total[k0][sub : sub + 1]
            p0 = value.astype(BF16).astype(F32)
            p1 = (value - p0).astype(BF16).astype(F32)
            left[0:4, at] = hit * p0
            left[4:8, at] = hit * p1
            left[8:12, at] = hit * (value - p0 - p1)
    got = dot_nt(left[...].astype(BF16), onehot[...])
    totals[...] = got[0:4] + got[4:8] + got[8:12]
    plane_totals = (totals, totals_in, s_total, r_total)
    start_all(32, plane_copy, *plane_totals)
    for k0 in range(8):
        half = (k0 // 4) * 64
        power_ref[pl.ds(k0, 8, stride=8), :] = total[k0 % 4][:, half : half + 64]
    all_counts = wait_column(*column_counts)
    totals_plane[...] = wait_plane(*plane_totals)
    column_totals = (totals_plane, totals_z, s_totalz, r_totalz)
    start_all(8, column_copy, *column_totals)
    sent_all(32, plane_copy, *plane_counts)
    sent_all(8, column_copy, *column_counts)
    sent_all(16, sum_copy)
    sent_all(32, plane_copy, *plane_totals)
    for k0 in range(4):
        pair_copy(k0).wait_send()
    spectrum_ref[...] = wait_column(*column_totals) / all_counts
    sent_all(8, column_copy, *column_totals)


def tail_call(grid, bins):
    dma = pltpu.SemaphoreType.DMA
    small = (4, 128)
    return pl.pallas_call(
        tail_kernel,
        out_shape=(jax.ShapeDtypeStruct((64, 64), F32), jax.ShapeDtypeStruct((4, 128), F32)),
        in_specs=[VMEM_SPEC] * 2,
        out_specs=(VMEM_SPEC,) * 2,
        scratch_shapes=[
            pltpu.VMEM((256, 1024), BF16),
            pltpu.VMEM((256, 1024), BF16),
            pltpu.VMEM((256, 256), BF16),
            pltpu.VMEM((256, 256), BF16),
            pltpu.VMEM((8, 2, 128, 128), F32),
            pltpu.VMEM((128, 128), F32),
            pltpu.VMEM((128, 4096), BF16),
            pltpu.VMEM((16, 4096), F32),
            pltpu.VMEM((2, 4, 2, 8, 8, 128), F32),
            pltpu.VMEM((4, 2, 8, 8, 128), F32),
            pltpu.VMEM((16, 4, 8, 128), F32),
            pltpu.VMEM((16, 4, 8, 128), F32),
            pltpu.VMEM(small, F32),
            pltpu.VMEM((32,) + small, F32),
            pltpu.VMEM((8,) + small, F32),
            pltpu.VMEM(small, F32),
            pltpu.VMEM(small, F32),
            pltpu.VMEM((32,) + small, F32),
            pltpu.VMEM((8,) + small, F32),
            pltpu.VMEM(small, F32),
            dma((4,)), dma((4,)), dma((16,)), dma((16,)),
            dma((32,)), dma((32,)), dma((32,)), dma((32,)),
            dma((8,)), dma((8,)), dma((8,)), dma((8,)),
        ],
        compiler_params=pltpu.CompilerParams(collective_id=1, has_side_effects=True),
    )(grid, bins)


def per_device(visibility, tile_of, u_within, v_cell, kernel_index, kernel, live_count, bin_map):
    merged = gather_call(
        live_count.T, visibility, tile_of.transpose(0, 2, 1), u_within, v_cell, kernel_index
    )
    grid = grid_call(merged, kernel.T)
    power, spectrum = tail_call(grid, bin_map)
    return power, spectrum.reshape(NBINS)


def solution(mesh):
    return jax.shard_map(
        per_device,
        mesh=mesh,
        in_specs=(
            P(None, "freq", "base"),
            P("freq", "base", None),
            P("freq", "base"),
            P("freq", "base"),
            P(None, "freq", "base"),
            P(),
            P("freq", "base"),
            P("base", None),
        ),
        out_specs=(P("freq", "base"), P()),
        check_vma=False,
    )
```

time: 163 us -> 70.8 us (0.43)
  blocking collectives: 109 us -> 0 us
  Pallas kernels: 24.3 us -> 67.2 us
  starting transfers between devices: 12.8 us -> 0 us
  waiting for transfers between devices: 10.5 us -> 0 us
  local copies, waits for them, and re-layouts: 4.29 us -> 2.63 us
    psum x1 -> x0, blocking collectives: 74 us -> none  [per_device(): sums = lax.psum(sums, AXES)]
    pallas_call x1, Pallas kernels: 2.26 us -> 30.2 us  [tail_call(): pl.pallas_call(tail_kernel, out_shape=(jax.ShapeDtypeStruct((64, 64), F32...]
    all_gather x1 -> x0, blocking collectives: 25.3 us -> none  [per_device(): got = lax.all_gather(mine, 'base_1')]
    pallas_call x2, Pallas kernels: 22 us -> 37 us  [the longest x1 19.2 us: grid_call(): pl.pallas_call(grid_kernel, out_shape=jax.ShapeDtypeStruct((1040, 256), F...]
    all_to_all x1 -> x0, starting transfers between devices: 12.8 us -> none  [per_device(): pieces = lax.all_to_all(pieces, ('base_0',) + FREQ, 0, 0, tiled=True)]
    all_to_all x1 -> x0, waiting for transfers between devices: 10.5 us -> none  [per_device(): pieces = lax.all_to_all(pieces, ('base_0',) + FREQ, 0, 0, tiled=True)]
    all_to_all x1 -> x0, blocking collectives: 9.47 us -> none  [per_device(): mine = lax.all_to_all(binned, 'base_0', 0, 0, tiled=True)]
    unnamed x7 -> x2, local copies, waits for them, and re-layouts: 3.5 us -> 2.63 us
  transfers between devices with their start and end apart: 1 -> 0, of which waited for: 1 -> 0; matrix products, arithmetic and copies ran while one was open for 1% -> 0% of each run, Pallas kernels for 0% -> 0%
where the time goes in v2:
time: 70.8 us; the launch traced here: 70.5 us
  Pallas kernels  67.2 us (95%)
  local copies, waits for them, and re-layouts  2.63 us (4%)
    pallas_call x1, Pallas kernels, tail_call(): pl.pallas_call(tail_kernel, out_shape=(jax.ShapeDtypeStruct((64, 64), F32...  30.2 us
    pallas_call x1, Pallas kernels, grid_call(): pl.pallas_call(grid_kernel, out_shape=jax.ShapeDtypeStruct((1040, 256), F...  19.2 us
    pallas_call x1, Pallas kernels, gather_call(): pl.pallas_call(gather_kernel, out_shape=jax.ShapeDtypeStruct((16, 48, 128...  17.8 us
    unnamed x2, local copies, waits for them, and re-layouts  2.63 us

profile of v2, /device:TPU:1, one launch (start us, length us, event | category | flops | bytes accessed | tf_op | source)
XLA Modules:
  0.0 70.5 jit_solution(6957328638208028722)
XLA Ops:
  0.6 17.8 %shard_map.95.merged = f32[16,48,128]{2,1,0:T(8,128)} custom-call(s32[1,2]{1,0:T(1,128)} %bitcast.7, f32[2,2,512]{2,1,0:T(2,128)} %vis_ref.1, s32[2,1,512]{2,1,0:T(1,128)} %bitcast.4, s32[2,512]{1,0:T(2,128)} %within_ref.1, s32[2,512]{1,0:T(2,128)} %vcell_ref.1, s32[2,2,512]{2,1,0:T(2,128)} %kidx_ref.1), custom_call_target="tpu_custom_call" | custom-call | tf_op jit(solution)/shard_map/pallas_call | solution.py:218
  18.4 19.2 %shard_map.96.grid_ref = f32[1040,256]{1,0:T(8,128)} custom-call(f32[16,48,128]{2,1,0:T(8,128)} %shard_map.95.merged, f32[8,128]{1,0:T(8,128)} %bitcast.5), custom_call_target="tpu_custom_call" | custom-call | tf_op jit(solution)/shard_map/pallas_call | solution.py:365
  37.7 30.2 %shard_map.97 = (f32[64,64]{1,0:T(8,128)}, f32[4,128]{1,0:T(4,128)}) custom-call(f32[1040,256]{1,0:T(8,128)} %shard_map.96.grid_ref, s32[64,1024]{1,0:T(8,128)} %bins_ref.1), custom_call_target="tpu_custom_call" | custom-call | tf_op jit(solution)/shard_map/pallas_call | solution.py:629
  67.9 1.4 %copy.12 = f32[64,64]{1,0:T(8,128)} copy(f32[64,64]{1,0:T(8,128)} %get-tuple-element.8) | data formatting | bytes 32768
  69.3 1.3 %copy.13 = f32[512]{0:T(512)} copy(f32[512]{0:T(512)} %bitcast.6) | data formatting | bytes 4096

commit v3 on v2

--- a/solution.py
+++ b/solution.py
@@ -15,11 +15,13 @@
 SLOTS = 512
 TILES = 16
 BLOCKS = 128
+GROUP = 4
 F32 = jnp.float32
 BF16 = jnp.bfloat16
 I32 = jnp.int32
 MESH = pl.DeviceIdType.MESH
 VMEM_SPEC = pl.BlockSpec(memory_space=pltpu.VMEM)
+LIMIT = 16 * 1024 * 1024
 NORM = 1.0 / (32 * 8192)
 
 
@@ -112,9 +114,59 @@
 
 
 def gather_kernel(
-    live_ref, vis_ref, tile_ref, within_ref, vcell_ref, kidx_ref, out_ref, packed, got, send, land, relay, local
+    live_hbm,
+    vis_hbm,
+    tile_hbm,
+    within_hbm,
+    vcell_hbm,
+    kidx_hbm,
+    kernel_hbm,
+    bins_ref,
+    out_ref,
+    kernel_ref,
+    used_ref,
+    phase_ref,
+    matrix_ref,
+    twiddle_ref,
+    onehot_ref,
+    hit_ref,
+    counts_ref,
+    packed,
+    got,
+    bins,
+    turned,
+    live_ref,
+    vis_ref,
+    tile_ref,
+    within_ref,
+    vcell_ref,
+    kidx_ref,
+    send,
+    land,
+    relay,
+    local,
+    fetched,
 ):
+    inputs = (
+        (live_hbm, live_ref),
+        (tile_hbm, tile_ref),
+        (vis_hbm, vis_ref),
+        (within_hbm, within_ref),
+        (vcell_hbm, vcell_ref),
+        (kidx_hbm, kidx_ref),
+        (kernel_hbm, kernel_ref),
+    )
+    loads = [
+        pltpu.make_async_copy(source, place, fetched.at[index])
+        for index, (source, place) in enumerate(inputs)
+    ]
+    for load in loads:
+        load.start()
     h, z = places()
+    freq = lax.axis_index("freq")
+    at = pl.multiple_of((freq // 2) * 128, 128)
+    fetch = pltpu.make_async_copy(bins_ref.at[:, pl.ds(at, 128)], bins, fetched.at[7])
+    fetch.start()
     hops = (1, -1, 2, -2)
 
     def device(side, step):
@@ -127,9 +179,12 @@
         pl.semaphore_signal(barrier, 1, device_id=device(1 - h, step), device_id_type=MESH)
 
     upper = (iota((SLOTS, SLOTS), 0) < iota((SLOTS, SLOTS), 1)).astype(F32).astype(BF16)
+    for load in loads:
+        load.wait()
     for ch in range(2):
+        live = live_ref[0:1, ch : ch + 1]
         parts = bin_channel(
-            ch, z, vis_ref, tile_ref, within_ref, vcell_ref, kidx_ref, live_ref[0, ch], upper
+            ch, z, vis_ref, tile_ref, within_ref, vcell_ref, kidx_ref, live, upper
         )
         for index, part in enumerate(parts):
             packed[ch, 12 * index : 12 * index + 6] = part[:6, :128]
@@ -169,6 +224,11 @@
         copy.start()
     own = pltpu.make_async_copy(packed.at[h], got.at[z, h], local)
     own.start()
+
+    column_tables(z, kernel_ref, phase_ref)
+    row_tables(matrix_ref, twiddle_ref)
+    fetch.wait()
+    bin_tables(freq % 2, bins, turned, onehot_ref, hit_ref, counts_ref)
 
     relays = []
 
@@ -212,60 +272,18 @@
             for p in range(1, 8):
                 block = jnp.where(group == p, got[(p - i) % 8, half], block)
             out_ref[half * 8 + i] = block
-
-
-def gather_call(live, visibility, tile, within, column, kernel_index):
-    return pl.pallas_call(
-        gather_kernel,
-        out_shape=jax.ShapeDtypeStruct((16, 48, 128), F32),
-        in_specs=[pl.BlockSpec(memory_space=pltpu.SMEM)] + [VMEM_SPEC] * 5,
-        out_specs=VMEM_SPEC,
-        scratch_shapes=[
-            pltpu.VMEM((2, 48, 128), F32),
-            pltpu.VMEM((8, 2, 48, 128), F32),
-            pltpu.SemaphoreType.DMA((9,)),
-            pltpu.SemaphoreType.DMA((8, 2)),
-            pltpu.SemaphoreType.DMA((6,)),
-            pltpu.SemaphoreType.DMA,
-        ],
-        compiler_params=pltpu.CompilerParams(collective_id=0, has_side_effects=True),
-    )(live, visibility, tile, within, column, kernel_index)
-
-
-def grid_kernel(
-    merged,
-    kernel_ref,
-    grid_ref,
-    ec_ref,
-    es_ref,
-    pc_ref,
-    ps_ref,
-    wh_a,
-    wl_a,
-    rh_a,
-    rl_a,
-    wh_b,
-    wl_b,
-    rh_b,
-    rl_b,
-    count_vmem,
-    count_smem,
-    order,
-    sem,
-):
-    _, z = places()
-    used = (merged[...].reshape(768, 128) != 0.0).astype(F32).astype(BF16)
-    counts = dot_nt(jnp.ones((8, 128), F32).astype(BF16), used)
-    count_vmem[...] = counts.astype(I32)
-    copy = pltpu.make_async_copy(count_vmem, count_smem, sem)
-    copy.start()
-
-    l_row = iota((128, 128), 0)
+    nonzero = (out_ref[...].reshape(768, 128) != 0.0).astype(F32).astype(BF16)
+    found = dot_nt(jnp.ones((8, 128), F32).astype(BF16), nonzero).astype(BF16)
+    row, block = iota((768, 128), 0), iota((768, 128), 1)
+    first = ((block >> 6) * 8 + (block & 7)) * 48 + ((block >> 3) & 7) * 6
+    pick = ((row == first) | (row == first + 1)).astype(F32).astype(BF16)
+    used_ref[...] = dot_nn(found, pick).astype(I32)
+
+
+def column_tables(z, kernel_ref, phase_ref):
+    l_row, lane = iota((128, 128), 0), iota((128, 128), 1)
     l_val = (l_row & 63) + (l_row >> 6) * 512 + z * 64
-    lane = iota((128, 128), 1)
-    ec, es = cis(l_val * lane, G)
-    ec_ref[...] = ec
-    es_ref[...] = es
+    phase_ref[0], phase_ref[1] = cis(l_val * lane, G)
     zr, zi = cis(l_val, G)
     kern = kernel_ref[...]
     pr = jnp.broadcast_to(kern[7:8], (128, 128))
@@ -273,27 +291,101 @@
     for s in range(6, -1, -1):
         pr, pi = cmul(pr, pi, zr, zi)
         pr = pr + kern[s : s + 1]
-    pc_ref[...] = pr
-    ps_ref[...] = pi
+    phase_ref[2] = pr
+    phase_ref[3] = pi
+
+
+def row_tables(matrix_ref, twiddle_ref):
+    row, lane = iota((128, 128), 0), iota((128, 128), 1)
+    fc, fs = cis(row * lane, 128)
+    for quarter, value in ((0, fc), (1, -fs), (2, fs), (3, fc)):
+        down, right = (quarter >> 1) * 128, (quarter & 1) * 128
+        for part, half in enumerate(split2(value)):
+            matrix_ref[part, down : down + 128, right : right + 128] = half
+    tr, ti = cis(row, G)
+    ar, ai = tr, ti
+    for k0 in range(1, 8):
+        twiddle_ref[k0 - 1, 0] = ar
+        twiddle_ref[k0 - 1, 1] = ai
+        if k0 < 7:
+            ar, ai = cmul(ar, ai, tr, ti)
+
+
+def bin_tables(core, bins, turned, onehot_ref, hit_ref, counts_ref):
+    full = jnp.concatenate([bins[...].astype(F32), jnp.zeros((64, 128), F32)], axis=0)
+    turned[...] = pltpu.roll(full, core * 64, 1).T
+    row128, high_row, lane8 = iota((128, 128), 0), iota((4, 128), 0), iota((8, 128), 1)
+    for k0 in range(4):
+        ours = turned[pl.ds(k0, 8, stride=8), :]
+        other = turned[pl.ds(k0 + 4, 8, stride=8), :]
+        both = jnp.where(lane8 < 64, ours, pltpu.roll(other, 64, 1)).astype(I32)
+        for sub in range(8):
+            found = both[sub : sub + 1]
+            at = slice(128 * (8 * k0 + sub), 128 * (8 * k0 + sub) + 128)
+            onehot_ref[:, at] = (row128 == (found & 127)).astype(F32).astype(BF16)
+            hit_ref[:, at] = ((found >> 7) == high_row).astype(F32)
+    counts_ref[...] = dot_nt(hit_ref[...].astype(BF16), onehot_ref[...])
+
+
+def gather_call(*args):
+    return pl.pallas_call(
+        gather_kernel,
+        out_shape=(
+            jax.ShapeDtypeStruct((16, 48, 128), F32),
+            jax.ShapeDtypeStruct((8, 128), F32),
+            jax.ShapeDtypeStruct((8, 128), I32),
+            jax.ShapeDtypeStruct((4, 128, 128), F32),
+            jax.ShapeDtypeStruct((2, 256, 256), BF16),
+            jax.ShapeDtypeStruct((7, 2, 128, 128), F32),
+            jax.ShapeDtypeStruct((128, 4096), BF16),
+            jax.ShapeDtypeStruct((4, 4096), F32),
+            jax.ShapeDtypeStruct((4, 128), F32),
+        ),
+        in_specs=[pl.BlockSpec(memory_space=pltpu.HBM)] * 8,
+        out_specs=(VMEM_SPEC,) * 9,
+        scratch_shapes=[
+            pltpu.VMEM((2, 48, 128), F32),
+            pltpu.VMEM((8, 2, 48, 128), F32),
+            pltpu.VMEM((64, 128), I32),
+            pltpu.VMEM((128, 128), F32),
+            pltpu.VMEM((1, 2), I32),
+            pltpu.VMEM((2, 2, SLOTS), F32),
+            pltpu.VMEM((2, 1, SLOTS), I32),
+            pltpu.VMEM((2, SLOTS), I32),
+            pltpu.VMEM((2, SLOTS), I32),
+            pltpu.VMEM((2, 2, SLOTS), I32),
+            pltpu.SemaphoreType.DMA((9,)),
+            pltpu.SemaphoreType.DMA((8, 2)),
+            pltpu.SemaphoreType.DMA((6,)),
+            pltpu.SemaphoreType.DMA,
+            pltpu.SemaphoreType.DMA((8,)),
+        ],
+        compiler_params=pltpu.CompilerParams(
+            collective_id=0, has_side_effects=True, vmem_limit_bytes=LIMIT
+        ),
+    )(*(pltpu.with_memory_space_constraint(x, pltpu.HBM) for x in args))
+
+
+def grid_kernel(merged, used_ref, phase_ref, kernel_ref, grid_ref, wbuf, rbuf, used, order, sem):
+    copy = pltpu.make_async_copy(used_ref, used, sem)
+    copy.start()
     sub = iota((8, 128), 0)
     ct_r, ct_i = cis(sub * iota((8, 128), 1), 8)
     grid_ref[...] = jnp.zeros_like(grid_ref)
-    for ref in (wh_b, wl_b, rh_b, rl_b):
-        ref[...] = jnp.zeros_like(ref)
-
+    for slot in range(2):
+        for i in range(GROUP):
+            rbuf[slot, i, 80:160, 128:256] = jnp.zeros((80, 128), BF16)
     copy.wait()
 
     def list_step(b, n):
         order[n] = b
-        first = ((b >> 6) * 8 + (b & 7)) * 48 + ((b >> 3) & 7) * 6
-        found = count_smem[0, first] + count_smem[0, first + 1]
-        return n + jnp.where(found > 0, 1, 0)
-
-    total = lax.fori_loop(0, BLOCKS, list_step, 0, unroll=8)
-    order[total] = BLOCKS
-    order[total + 1] = BLOCKS
-
-    def build(bid, wh, wl, rh, rl):
+        return n + jnp.where(used[0, b] > 0, 1, 0)
+
+    total = lax.fori_loop(0, BLOCKS, list_step, 0, unroll=16)
+    for i in range(GROUP):
+        order[total + i] = BLOCKS
+
+    def build(bid, slot, i):
         which = ((bid >> 6) & 1) * 8 + (bid & 7)
         first = ((bid >> 3) & 7) * 6
         keep = jnp.where(bid < BLOCKS, 1.0, 0.0)
@@ -314,10 +406,10 @@
             res, ims = [], []
             for lg in (2 * pair, 2 * pair + 1):
                 at = slice(8 * lg, 8 * lg + 8)
-                er = take_lanes(ec_ref[at], index_d)
-                ei = take_lanes(es_ref[at], index_d)
-                qr = take_lanes(pc_ref[at], index_v)
-                qi = take_lanes(ps_ref[at], index_v)
+                er = take_lanes(phase_ref[0, at], index_d)
+                ei = take_lanes(phase_ref[1, at], index_d)
+                qr = take_lanes(phase_ref[2, at], index_v)
+                qi = take_lanes(phase_ref[3, at], index_v)
                 ar, ai = cmul(er, ei, qr, qi)
                 ar, ai = cmul(ar, ai, cr, ci)
                 res.append(ar)
@@ -325,8 +417,8 @@
             for base, values in ((0, res), (128, ims)):
                 hi, lo = split2(jnp.concatenate(values, axis=0))
                 at = slice(base + 16 * pair, base + 16 * pair + 16)
-                wh[at] = hi
-                wl[at] = lo
+                wbuf[slot, i, at, 0:128] = hi
+                wbuf[slot, i, at, 128:256] = lo
         taps = take_lanes(kernel_ref[...], index_u)
         turned = jnp.take_along_axis(taps, (sub - w) & 7, axis=0, mode="promise_in_bounds")
         high = turned.astype(BF16).astype(F32)
@@ -339,49 +431,57 @@
                 hit = down == k
                 his.append(jnp.where(hit, high, zero))
                 los.append(jnp.where(hit, low, zero))
-            rh[16 * pair : 16 * pair + 16] = jnp.concatenate(his, axis=0).astype(BF16)
-            rl[16 * pair : 16 * pair + 16] = jnp.concatenate(los, axis=0).astype(BF16)
-
-    def place(bid, wh, wl, rh, rl):
-        res = dot_nt(rh[...], wh[...]) + dot_nt(rh[...], wl[...]) + dot_nt(rl[...], wh[...])
+            hi = jnp.concatenate(his, axis=0).astype(BF16)
+            at = slice(16 * pair, 16 * pair + 16)
+            rbuf[slot, i, at, 0:128] = hi
+            rbuf[slot, i, at, 128:256] = hi
+            at = slice(80 + 16 * pair, 80 + 16 * pair + 16)
+            rbuf[slot, i, at, 0:128] = jnp.concatenate(los, axis=0).astype(BF16)
+
+    def place(bid, slot, i):
+        res = dot_nt(rbuf[slot, i], wbuf[slot, i])
         start = pl.multiple_of(((bid >> 2) & 15) * 64, 64)
-        grid_ref[pl.ds(start, 80), :] += res
-
-    def step(pair, previous):
-        first, second = order[2 * pair], order[2 * pair + 1]
-        place(previous, wh_b, wl_b, rh_b, rl_b)
-        build(first, wh_a, wl_a, rh_a, rl_a)
-        place(first, wh_a, wl_a, rh_a, rl_a)
-        build(second, wh_b, wl_b, rh_b, rl_b)
-        return second
-
-    last = lax.fori_loop(0, (total + 1) >> 1, step, jnp.int32(BLOCKS))
-    place(last, wh_b, wl_b, rh_b, rl_b)
-
-def grid_call(merged, kernel_t):
-    w = pltpu.VMEM((256, 128), BF16)
-    r = pltpu.VMEM((80, 128), BF16)
-    t = pltpu.VMEM((128, 128), F32)
+        grid_ref[pl.ds(start, 80), :] += res[:80] + res[80:]
+
+    def fill(it, slot):
+        bids = tuple(order[GROUP * it + i] for i in range(GROUP))
+        for i in range(GROUP):
+            build(bids[i], slot, i)
+        return bids
+
+    def step(it, before):
+        slot = it & 1
+        for i in range(GROUP):
+            place(before[i], 1 - slot, i)
+        return fill(it, slot)
+
+    rounds = (total + GROUP - 1) // GROUP
+    last = lax.fori_loop(1, rounds, step, fill(0, 0))
+    slot = jnp.where(rounds > 0, (rounds - 1) & 1, 0)
+    for i in range(GROUP):
+        place(last[i], slot, i)
+
+
+def grid_call(merged, used, phase, kernel_t):
     return pl.pallas_call(
         grid_kernel,
         out_shape=jax.ShapeDtypeStruct((1040, 256), F32),
-        in_specs=[VMEM_SPEC] * 2,
+        in_specs=[VMEM_SPEC] * 4,
         out_specs=VMEM_SPEC,
         scratch_shapes=[
-            t, t, t, t,
-            w, w, r, r, w, w, r, r,
-            pltpu.VMEM((8, 768), I32),
-            pltpu.SMEM((8, 768), I32),
-            pltpu.SMEM((BLOCKS + 2,), I32),
+            pltpu.VMEM((2, GROUP, 256, 256), BF16),
+            pltpu.VMEM((2, GROUP, 160, 256), BF16),
+            pltpu.SMEM((8, 128), I32),
+            pltpu.SMEM((BLOCKS + GROUP,), I32),
             pltpu.SemaphoreType.DMA,
         ],
-    )(merged, kernel_t)
+        compiler_params=pltpu.CompilerParams(vmem_limit_bytes=LIMIT),
+    )(merged, used, phase, kernel_t)
 
 
 def tail_kernel(
-    grid_ref, bins_ref, power_ref, spectrum_ref,
-    bh_ref, bl_ref, mh_ref, ml_ref, tw_ref, turned, onehot, left,
-    piece, partner, summed, landed, counts, counts_in, counts_z, counts_plane, totals, totals_in, totals_z, totals_plane,
+    grid_ref, matrix_ref, tw_ref, onehot, hit_ref, counts, power_ref, spectrum_ref,
+    bh_ref, bl_ref, left, piece, partner, summed, landed, counts_in, counts_z, counts_plane, totals, totals_in, totals_z, totals_plane,
     s_pair, r_pair, s_sum, r_sum, s_count, r_count, s_total, r_total, s_countz, r_countz, s_totalz, r_totalz,
 ):
     h, z = places()
@@ -408,49 +508,6 @@
 
     lax.fori_loop(1, 32, greet_plane, 0)
     lax.fori_loop(1, 8, greet_column, 0)
-
-    row128, lane128 = iota((128, 128), 0), iota((128, 128), 1)
-    fc, fs = cis(row128 * lane128, 128)
-    for quarter, value in ((0, fc), (1, -fs), (2, fs), (3, fc)):
-        hi, lo = split2(value)
-        at = (
-            slice((quarter >> 1) * 128, (quarter >> 1) * 128 + 128),
-            slice((quarter & 1) * 128, (quarter & 1) * 128 + 128),
-        )
-        mh_ref[at] = hi
-        ml_ref[at] = lo
-    tr, ti = cis(row128, G)
-    ar, ai = tr, ti
-    for k0 in range(1, 8):
-        tw_ref[k0, 0] = ar
-        tw_ref[k0, 1] = ai
-        if k0 < 7:
-            ar, ai = cmul(ar, ai, tr, ti)
-
-    at = pl.multiple_of((freq // 2) * 128, 128)
-    bins = bins_ref[:, pl.ds(at, 128)].astype(F32)
-    bins = jnp.concatenate([bins, jnp.zeros((64, 128), F32)], axis=0)
-    bins = pltpu.roll(bins, core * 64, 1)
-    turned[...] = bins.T
-    high_row = iota((4, 128), 0)
-    lane8 = iota((8, 128), 1)
-    hits = []
-    for k0 in range(4):
-        ours = turned[pl.ds(k0, 8, stride=8), :]
-        other = turned[pl.ds(k0 + 4, 8, stride=8), :]
-        both = jnp.where(lane8 < 64, ours, pltpu.roll(other, 64, 1)).astype(I32)
-        for sub in range(8):
-            row = 8 * k0 + sub
-            found = both[sub : sub + 1]
-            at = slice(128 * row, 128 * row + 128)
-            onehot[:, at] = (row128 == (found & 127)).astype(F32).astype(BF16)
-            hit = ((found >> 7) == high_row).astype(F32)
-            left[12:16, at] = hit
-            left[0:4, at] = hit
-            left[4:8, at] = hit
-            left[8:12, at] = hit
-    got = dot_nt(left[...].astype(BF16), onehot[...])
-    counts[...] = got[12:16]
 
     root = math.sqrt(0.5)
     slot_of = (0, 2, 4, 6, 1, 3, 5, 7)
@@ -486,7 +543,7 @@
         for k0 in range(8):
             xr, xi = spectrum[k0]
             if k0:
-                xr, xi = cmul(xr, xi, tw_ref[k0, 0, at], tw_ref[k0, 1, at])
+                xr, xi = cmul(xr, xi, tw_ref[k0 - 1, 0, at], tw_ref[k0 - 1, 1, at])
             col = slice(128 * slot_of[k0], 128 * slot_of[k0] + 128)
             for base, value in ((0, xr), (128, xi)):
                 hi, lo = split2(value)
@@ -556,7 +613,7 @@
     low_half = iota((128, 128), 1) < 64
     for k0 in range(4):
         col = slice(256 * k0, 256 * k0 + 256)
-        full = dot_nn(mh_ref[...], bh_ref[:, col]) + dot_nn(mh_ref[...], bl_ref[:, col]) + dot_nn(ml_ref[...], bh_ref[:, col])
+        full = dot_nn(matrix_ref[0], bh_ref[:, col]) + dot_nn(matrix_ref[0], bl_ref[:, col]) + dot_nn(matrix_ref[1], bh_ref[:, col])
         power = (full[:128] * full[:128] + full[128:] * full[128:]) * NORM
         pa, pb = power[:, :128], power[:, 128:]
         ra, rb = pltpu.roll(pa, 64, 1), pltpu.roll(pb, 64, 1)
@@ -595,7 +652,7 @@
     for k0 in range(4):
         for sub in range(8):
             at = slice(128 * (8 * k0 + sub), 128 * (8 * k0 + sub) + 128)
-            hit = left[12:16, at]
+            hit = hit_ref[:, at]
             value = total[k0][sub : sub + 1]
             p0 = value.astype(BF16).astype(F32)
             p1 = (value - p0).astype(BF16).astype(F32)
@@ -623,28 +680,22 @@
     sent_all(8, column_copy, *column_totals)
 
 
-def tail_call(grid, bins):
+def tail_call(grid, matrix, twiddle, onehot, hit, counts):
     dma = pltpu.SemaphoreType.DMA
     small = (4, 128)
     return pl.pallas_call(
         tail_kernel,
         out_shape=(jax.ShapeDtypeStruct((64, 64), F32), jax.ShapeDtypeStruct((4, 128), F32)),
-        in_specs=[VMEM_SPEC] * 2,
+        in_specs=[VMEM_SPEC] * 6,
         out_specs=(VMEM_SPEC,) * 2,
         scratch_shapes=[
             pltpu.VMEM((256, 1024), BF16),
             pltpu.VMEM((256, 1024), BF16),
-            pltpu.VMEM((256, 256), BF16),
-            pltpu.VMEM((256, 256), BF16),
-            pltpu.VMEM((8, 2, 128, 128), F32),
-            pltpu.VMEM((128, 128), F32),
-            pltpu.VMEM((128, 4096), BF16),
             pltpu.VMEM((16, 4096), F32),
             pltpu.VMEM((2, 4, 2, 8, 8, 128), F32),
             pltpu.VMEM((4, 2, 8, 8, 128), F32),
             pltpu.VMEM((16, 4, 8, 128), F32),
             pltpu.VMEM((16, 4, 8, 128), F32),
-            pltpu.VMEM(small, F32),
             pltpu.VMEM((32,) + small, F32),
             pltpu.VMEM((8,) + small, F32),
             pltpu.VMEM(small, F32),
@@ -656,16 +707,25 @@
             dma((32,)), dma((32,)), dma((32,)), dma((32,)),
             dma((8,)), dma((8,)), dma((8,)), dma((8,)),
         ],
-        compiler_params=pltpu.CompilerParams(collective_id=1, has_side_effects=True),
-    )(grid, bins)
+        compiler_params=pltpu.CompilerParams(
+            collective_id=1, has_side_effects=True, vmem_limit_bytes=LIMIT
+        ),
+    )(grid, matrix, twiddle, onehot, hit, counts)
 
 
 def per_device(visibility, tile_of, u_within, v_cell, kernel_index, kernel, live_count, bin_map):
-    merged = gather_call(
-        live_count.T, visibility, tile_of.transpose(0, 2, 1), u_within, v_cell, kernel_index
+    merged, kernel_rows, used, phase, matrix, twiddle, onehot, hit, counts = gather_call(
+        live_count.T,
+        visibility,
+        tile_of.transpose(0, 2, 1),
+        u_within,
+        v_cell,
+        kernel_index,
+        kernel.T,
+        bin_map,
     )
-    grid = grid_call(merged, kernel.T)
-    power, spectrum = tail_call(grid, bin_map)
+    grid = grid_call(merged, used, phase, kernel_rows)
+    power, spectrum = tail_call(grid, matrix, twiddle, onehot, hit, counts)
     return power, spectrum.reshape(NBINS)
 
 

time: 70.8 us -> 60.2 us (0.85)
  Pallas kernels: 67.2 us -> 57.8 us
  local copies, waits for them, and re-layouts: 2.63 us -> 1.2 us
    pallas_call x1, Pallas kernels: 19.2 us -> 12.4 us  [grid_call(): pl.pallas_call(grid_kernel, out_shape=jax.ShapeDtypeStruct((1040, 256), F...]
    unnamed x2, local copies, waits for them, and re-layouts: 2.63 us -> 1.2 us
    pallas_call x1, Pallas kernels: 30.2 us -> 28.9 us  [tail_call(): pl.pallas_call(tail_kernel, out_shape=(jax.ShapeDtypeStruct((64, 64), F32...]
    pallas_call x1, Pallas kernels: 17.8 us -> 16.6 us  [gather_call(): pl.pallas_call(gather_kernel, out_shape=(jax.ShapeDtypeStruct((16, 48, 12...]
where the time goes in v3:
time: 60.2 us; the launch traced here: 59.7 us
  Pallas kernels  57.8 us (96%)
  local copies, waits for them, and re-layouts  1.2 us (2%)
  between operations  0.66 us (1%)
    pallas_call x1, Pallas kernels, tail_call(): pl.pallas_call(tail_kernel, out_shape=(jax.ShapeDtypeStruct((64, 64), F32...  28.9 us
    pallas_call x1, Pallas kernels, gather_call(): pl.pallas_call(gather_kernel, out_shape=(jax.ShapeDtypeStruct((16, 48, 12...  16.6 us
    pallas_call x1, Pallas kernels, grid_call(): pl.pallas_call(grid_kernel, out_shape=jax.ShapeDtypeStruct((1040, 256), F...  12.4 us

profile of v3, /device:TPU:1, one launch (start us, length us, event | category | flops | bytes accessed | tf_op | source)
XLA Modules:
  0.0 59.7 jit_solution(9832220251595050303)
XLA Ops:
  0.6 16.6 %shard_map.95 = (f32[16,48,128]{2,1,0:T(8,128)S(1)}, f32[8,128]{1,0:T(8,128)S(1)}, s32[8,128]{1,0:T(8,128)S(1)}, f32[4,128,128]{2,1,0:T(8,128)S(1)}, bf16[2,256,...) custom-call(s32[1,2]{1,0:T(1,128)} %bitcast.7, ...), custom_call_target="tpu_custom_call" | custom-call | tf_op jit(solution)/shard_map/pallas_call | solution.py:331
  17.2 12.4 %shard_map.96.grid_ref = f32[1040,256]{1,0:T(8,128)S(1)} custom-call(f32[16,48,128]{2,1,0:T(8,128)S(1)} %get-tuple-element.13.merged, s32[8,128]{1,0:T(8,128)S(1)} %get-tuple-element.14.used_ref, f32[4,128,128]{2,1,0:T(8,128)S(1)} %get-tuple-element.15.phase_ref, f32[8,128]{1,0:T(8,128)S(1)} %get-tuple-element.16.kernel_ref), custom_call_target="tpu_custom_call" | custom-call | tf_op jit(solution)/shard_map/pallas_call | solution.py:466
  29.6 28.9 %shard_map.97 = (f32[64,64]{1,0:T(8,128)S(1)}, f32[4,128]{1,0:T(4,128)S(1)}) custom-call(f32[1040,256]{1,0:T(8,128)S(1)} %shard_map.96.grid_ref, bf16[2,256,256]{2,1,0:T(8,128)(2,1)S(1)} %get-tuple-element.17.matrix_ref, f32[7,2,128,128]{3,2,1,0:T(8,128)S(1)} %get-tuple-element.18.tw_ref, bf16[128,4096]{1,0:T(8,128)(2,1)S(1)} %get-tuple-element.19.onehot, ...), custom_call_target="tpu_custom_call" | custom-call | tf_op jit(solution)/shard_map/pallas_call | solution.py:686
  58.5 0.6 %copy.12 = f32[64,64]{1,0:T(8,128)} copy(f32[64,64]{1,0:T(8,128)S(1)} %get-tuple-element.26) | data formatting | bytes 32768
  59.1 0.6 copy.13

commit v4 on v3

--- a/solution.py
+++ b/solution.py
@@ -16,6 +16,7 @@
 TILES = 16
 BLOCKS = 128
 GROUP = 4
+CHUNK = 16
 F32 = jnp.float32
 BF16 = jnp.bfloat16
 I32 = jnp.int32
@@ -402,23 +403,17 @@
         cr = take_lanes(ct_r, index_c)
         ci = take_lanes(ct_i, index_c)
         cr, ci = cmul(cr, ci, field(0) * keep, field(1) * keep)
-        for pair in range(8):
-            res, ims = [], []
-            for lg in (2 * pair, 2 * pair + 1):
-                at = slice(8 * lg, 8 * lg + 8)
-                er = take_lanes(phase_ref[0, at], index_d)
-                ei = take_lanes(phase_ref[1, at], index_d)
-                qr = take_lanes(phase_ref[2, at], index_v)
-                qi = take_lanes(phase_ref[3, at], index_v)
-                ar, ai = cmul(er, ei, qr, qi)
-                ar, ai = cmul(ar, ai, cr, ci)
-                res.append(ar)
-                ims.append(ai)
-            for base, values in ((0, res), (128, ims)):
-                hi, lo = split2(jnp.concatenate(values, axis=0))
-                at = slice(base + 16 * pair, base + 16 * pair + 16)
-                wbuf[slot, i, at, 0:128] = hi
-                wbuf[slot, i, at, 128:256] = lo
+        for chunk in range(0, 16, CHUNK):
+            rows = [slice(8 * lg, 8 * lg + 8) for lg in range(chunk, chunk + CHUNK)]
+            phase = [(take_lanes(phase_ref[0, at], index_d), take_lanes(phase_ref[1, at], index_d)) for at in rows]
+            taps = [(take_lanes(phase_ref[2, at], index_v), take_lanes(phase_ref[3, at], index_v)) for at in rows]
+            done = [cmul(*cmul(*a, *b), cr, ci) for a, b in zip(phase, taps)]
+            for pair in range(CHUNK // 2):
+                for part in range(2):
+                    hi, lo = split2(jnp.concatenate([done[2 * pair][part], done[2 * pair + 1][part]], axis=0))
+                    start = part * 128 + 8 * chunk + 16 * pair
+                    wbuf[slot, i, start : start + 16, 0:128] = hi
+                    wbuf[slot, i, start : start + 16, 128:256] = lo
         taps = take_lanes(kernel_ref[...], index_u)
         turned = jnp.take_along_axis(taps, (sub - w) & 7, axis=0, mode="promise_in_bounds")
         high = turned.astype(BF16).astype(F32)
@@ -481,33 +476,34 @@
 
 def tail_kernel(
     grid_ref, matrix_ref, tw_ref, onehot, hit_ref, counts, power_ref, spectrum_ref,
-    bh_ref, bl_ref, left, piece, partner, summed, landed, counts_in, counts_z, counts_plane, totals, totals_in, totals_z, totals_plane,
-    s_pair, r_pair, s_sum, r_sum, s_count, r_count, s_total, r_total, s_countz, r_countz, s_totalz, r_totalz,
+    bh_ref, bl_ref, left, piece, partner, summed, landed, counts_in, counts_z, counts_plane,
+    totals, totals_in, totals_z, totals_plane, sems,
 ):
     h, z = places()
     freq = lax.axis_index("freq")
     quad, core = freq // 2, freq % 2
     me = h * 16 + freq
     me_pair = h * 8 + quad
-
-    def plane_device(index):
-        return {"freq": index % 16, "base": (index // 16) * 8 + z}
-
-    def column_device(index):
-        return {"freq": freq, "base": h * 8 + index}
+    far_first = (4, 3, 5, 2, 6, 1, 7)
+
+    def chip(index, to_core):
+        return {"freq": (index % 8) * 2 + to_core, "base": (index // 8) * 8 + z}
+
+    def column(step, to_core):
+        return {"freq": quad * 2 + to_core, "base": h * 8 + (z + step) % 8}
 
     barrier = pltpu.get_barrier_semaphore()
 
-    def greet_plane(k, _):
-        pl.semaphore_signal(barrier, 1, device_id=plane_device((me + k) % 32), device_id_type=MESH)
-        return 0
-
-    def greet_column(k, _):
-        pl.semaphore_signal(barrier, 1, device_id=column_device((z + k) % 8), device_id_type=MESH)
-        return 0
-
-    lax.fori_loop(1, 32, greet_plane, 0)
-    lax.fori_loop(1, 8, greet_column, 0)
+    def greet(device):
+        pl.semaphore_signal(barrier, 1, device_id=device, device_id_type=MESH)
+
+    for step in far_first:
+        for to_core in range(2):
+            greet(column(step, to_core))
+    for k in range(1, 16):
+        for to_core in range(2):
+            greet(chip((me_pair + k) % 16, to_core))
+    greet(chip(me_pair, 1 - core))
 
     root = math.sqrt(0.5)
     slot_of = (0, 2, 4, 6, 1, 3, 5, 7)
@@ -549,67 +545,6 @@
                 hi, lo = split2(value)
                 bh_ref[base + 16 * rows : base + 16 * rows + 16, col] = hi
                 bl_ref[base + 16 * rows : base + 16 * rows + 16, col] = lo
-    pl.semaphore_wait(barrier, 38)
-
-    def plane_copy(k, buf, slots, s, r):
-        peer = (me + k) % 32
-        return pltpu.make_async_remote_copy(
-            src_ref=buf, dst_ref=slots.at[me], send_sem=s.at[k], recv_sem=r.at[me],
-            device_id=plane_device(peer), device_id_type=MESH,
-        )
-
-    def column_copy(k, buf, slots, s, r):
-        peer = (z + k) % 8
-        return pltpu.make_async_remote_copy(
-            src_ref=buf, dst_ref=slots.at[z], send_sem=s.at[k], recv_sem=r.at[z],
-            device_id=column_device(peer), device_id_type=MESH,
-        )
-
-    def start_all(count, make, *args):
-        def body(k, _):
-            make(k, *args).start()
-            return 0
-
-        lax.fori_loop(1, count, body, 0)
-
-    def wait_plane(buf, slots, s, r):
-        def body(k, total):
-            source = (me + k) % 32
-            pltpu.make_async_remote_copy(
-                src_ref=buf, dst_ref=slots.at[source], send_sem=s.at[k], recv_sem=r.at[source],
-                device_id=plane_device(source), device_id_type=MESH,
-            ).wait_recv()
-            return total + slots[source]
-
-        return lax.fori_loop(1, 32, body, buf[...])
-
-    def wait_column(buf, slots, s, r):
-        def body(k, total):
-            source = (z + k) % 8
-            pltpu.make_async_remote_copy(
-                src_ref=buf, dst_ref=slots.at[source], send_sem=s.at[k], recv_sem=r.at[source],
-                device_id=column_device(source), device_id_type=MESH,
-            ).wait_recv()
-            return total + slots[source]
-
-        return lax.fori_loop(1, 8, body, buf[...])
-
-    def sent_all(count, make, *args):
-        def body(k, _):
-            make(k, *args).wait_send()
-            return 0
-
-        lax.fori_loop(1, count, body, 0)
-
-    plane_counts = (counts, counts_in, s_count, r_count)
-    start_all(32, plane_copy, *plane_counts)
-
-    def pair_copy(k0):
-        return pltpu.make_async_remote_copy(
-            src_ref=piece.at[1 - core, k0], dst_ref=partner.at[k0], send_sem=s_pair.at[k0], recv_sem=r_pair.at[k0],
-            device_id={"freq": quad * 2 + 1 - core}, device_id_type=MESH,
-        )
-
     low_half = iota((128, 128), 1) < 64
     for k0 in range(4):
         col = slice(256 * k0, 256 * k0 + 256)
@@ -621,34 +556,87 @@
             block = block.reshape(8, 2, 8, 128)
             for cc in range(2):
                 piece[cc, k0, side] = block[:, cc]
-        pair_copy(k0).start()
+
+    pl.semaphore_wait(barrier, 45)
+
+    def remote(source, target, number, device):
+        return pltpu.make_async_remote_copy(
+            src_ref=source, dst_ref=target, send_sem=sems.at[2 * number], recv_sem=sems.at[2 * number + 1],
+            device_id=device, device_id_type=MESH,
+        )
+
+    def whole(ref, count, number):
+        return remote(ref.at[0:count], ref.at[0:count], number, chip(me_pair, 1 - core))
+
+    pair = remote(piece.at[1 - core], partner, 0, chip(me_pair, 1 - core))
+    pair.start()
+
+    def plane_send(buf, slots, number):
+        @pl.when(core == 0)
+        def _():
+            remote(buf, slots.at[me], number, chip(me_pair, 1)).start()
+
+        for k in range(1, 16):
+            remote(buf, slots.at[me], number, chip((me_pair + k) % 16, 1)).start()
+
+    def plane_sum(buf, slots, result, number):
+        slots[me] = buf[...]
+        whole(slots, 31, number).wait_recv()
+        total = slots[0]
+        for index in range(1, 32):
+            total = total + slots[index]
+        result[...] = total
+
+    def column_send(buf, slots, number):
+        for step in far_first:
+            for to_core in range(2):
+                remote(buf, slots.at[z], number, column(step, to_core)).start()
+        remote(buf, slots.at[z], number, chip(me_pair, 0)).start()
+
+    def column_sum(buf, slots, number):
+        @pl.when(core == 0)
+        def _():
+            whole(slots, 8, number).wait_recv()
+
+        @pl.when(core == 1)
+        def _():
+            slots[z] = buf[...]
+            whole(slots, 7, number).wait_recv()
+
+        total = slots[0]
+        for index in range(1, 8):
+            total = total + slots[index]
+        return total
+
+    def plane_sent(slots, number):
+        @pl.when(core == 0)
+        def _():
+            whole(slots, 16, number).wait_send()
+
+        @pl.when(core == 1)
+        def _():
+            whole(slots, 15, number).wait_send()
+
+    plane_send(counts, counts_in, 2)
+    pair.wait_recv()
     for k0 in range(4):
-        pair_copy(k0).wait_recv()
         for side in range(2):
             for q in range(8):
                 summed[side * 8 + q, k0] = piece[core, k0, side, q] + partner[k0, side, q]
-
-    def sum_copy(k):
+    for k in range(1, 16):
         peer = (me_pair + k) % 16
-        return pltpu.make_async_remote_copy(
-            src_ref=summed.at[peer], dst_ref=landed.at[me_pair], send_sem=s_sum.at[k], recv_sem=r_sum.at[me_pair],
-            device_id={"freq": (peer % 8) * 2 + core, "base": (peer // 8) * 8 + z}, device_id_type=MESH,
-        )
-
-    start_all(16, sum_copy)
-    counts_plane[...] = wait_plane(*plane_counts)
-    column_counts = (counts_plane, counts_z, s_countz, r_countz)
-    start_all(8, column_copy, *column_counts)
-
-    def wait_sum(k, total):
-        source = (me_pair + k) % 16
-        pltpu.make_async_remote_copy(
-            src_ref=summed.at[source], dst_ref=landed.at[source], send_sem=s_sum.at[k], recv_sem=r_sum.at[source],
-            device_id={"freq": (source % 8) * 2 + core, "base": (source // 8) * 8 + z}, device_id_type=MESH,
-        ).wait_recv()
-        return total + landed[source]
-
-    total = lax.fori_loop(1, 16, wait_sum, summed[me_pair])
+        remote(summed.at[peer], landed.at[me_pair], 1, chip(peer, core)).start()
+    landed[me_pair] = summed[me_pair]
+
+    @pl.when(core == 1)
+    def _():
+        plane_sum(counts, counts_in, counts_plane, 2)
+        column_send(counts_plane, counts_z, 3)
+
+    whole(landed, 15, 1).wait_recv()
+    total = landed[0]
+    for index in range(1, 16):
+        total = total + landed[index]
     for k0 in range(4):
         for sub in range(8):
             at = slice(128 * (8 * k0 + sub), 128 * (8 * k0 + sub) + 128)
@@ -659,29 +647,37 @@
             left[0:4, at] = hit * p0
             left[4:8, at] = hit * p1
             left[8:12, at] = hit * (value - p0 - p1)
+            left[12:16, at] = jnp.zeros((4, 128), F32)
     got = dot_nt(left[...].astype(BF16), onehot[...])
     totals[...] = got[0:4] + got[4:8] + got[8:12]
-    plane_totals = (totals, totals_in, s_total, r_total)
-    start_all(32, plane_copy, *plane_totals)
+    plane_send(totals, totals_in, 4)
     for k0 in range(8):
         half = (k0 // 4) * 64
         power_ref[pl.ds(k0, 8, stride=8), :] = total[k0 % 4][:, half : half + 64]
-    all_counts = wait_column(*column_counts)
-    totals_plane[...] = wait_plane(*plane_totals)
-    column_totals = (totals_plane, totals_z, s_totalz, r_totalz)
-    start_all(8, column_copy, *column_totals)
-    sent_all(32, plane_copy, *plane_counts)
-    sent_all(8, column_copy, *column_counts)
-    sent_all(16, sum_copy)
-    sent_all(32, plane_copy, *plane_totals)
-    for k0 in range(4):
-        pair_copy(k0).wait_send()
-    spectrum_ref[...] = wait_column(*column_totals) / all_counts
-    sent_all(8, column_copy, *column_totals)
+    all_counts = column_sum(counts_plane, counts_z, 3)
+
+    @pl.when(core == 1)
+    def _():
+        plane_sum(totals, totals_in, totals_plane, 4)
+        column_send(totals_plane, totals_z, 5)
+
+    pair.wait_send()
+    whole(landed, 15, 1).wait_send()
+    plane_sent(counts_in, 2)
+    plane_sent(totals_in, 4)
+
+    @pl.when(core == 1)
+    def _():
+        whole(counts_in, 15, 3).wait_send()
+
+    spectrum_ref[...] = column_sum(totals_plane, totals_z, 5) / all_counts
+
+    @pl.when(core == 1)
+    def _():
+        whole(totals_in, 15, 5).wait_send()
 
 
 def tail_call(grid, matrix, twiddle, onehot, hit, counts):
-    dma = pltpu.SemaphoreType.DMA
     small = (4, 128)
     return pl.pallas_call(
         tail_kernel,
@@ -703,9 +699,7 @@
             pltpu.VMEM((32,) + small, F32),
             pltpu.VMEM((8,) + small, F32),
             pltpu.VMEM(small, F32),
-            dma((4,)), dma((4,)), dma((16,)), dma((16,)),
-            dma((32,)), dma((32,)), dma((32,)), dma((32,)),
-            dma((8,)), dma((8,)), dma((8,)), dma((8,)),
+            pltpu.SemaphoreType.DMA((12,)),
         ],
         compiler_params=pltpu.CompilerParams(
             collective_id=1, has_side_effects=True, vmem_limit_bytes=LIMIT

time: 60.2 us -> 52.3 us (0.87); the launches traced: 59.7 us -> 52.4 us
  Pallas kernels: 57.8 us -> 50.6 us
    pallas_call x1, Pallas kernels: 28.9 us -> 24.9 us  [tail_call(): pl.pallas_call(tail_kernel, out_shape=(jax.ShapeDtypeStruct((64, 64), F32...]
    pallas_call x1, Pallas kernels: 12.4 us -> 9.05 us  [grid_call(): pl.pallas_call(grid_kernel, out_shape=jax.ShapeDtypeStruct((1040, 256), F...]
where the time goes in v4:
time: 52.3 us; the launch traced here: 52.4 us
  Pallas kernels  50.6 us (97%)
  local copies, waits for them, and re-layouts  1.2 us (2%)
  between operations  0.66 us (1%)
    pallas_call x1, Pallas kernels, tail_call(): pl.pallas_call(tail_kernel, out_shape=(jax.ShapeDtypeStruct((64, 64), F32...  24.9 us
    pallas_call x1, Pallas kernels, gather_call(): pl.pallas_call(gather_kernel, out_shape=(jax.ShapeDtypeStruct((16, 48, 12...  16.6 us
    pallas_call x1, Pallas kernels, grid_call(): pl.pallas_call(grid_kernel, out_shape=jax.ShapeDtypeStruct((1040, 256), F...  9.05 us
    unnamed x2, local copies, waits for them, and re-layouts  1.2 us

profile of v4, /device:TPU:1, one launch (start us, length us, event | category | flops | bytes accessed | tf_op | source)
XLA Modules:
  0.0 52.4 jit_solution(7336360838036892467)
XLA Ops:
  0.6 16.6 %shard_map.95 = (f32[16,48,128]{2,1,0:T(8,128)S(1)}, f32[8,128]{1,0:T(8,128)S(1)}, s32[8,128]{1,0:T(8,128)S(1)}, f32[4,128,128]{2,1,0:T(8,128)S(1)}, bf16[2,256,...) custom-call(s32[1,2]{1,0:T(1,128)} %bitcast.7, ...), custom_call_target="tpu_custom_call" | custom-call | tf_op jit(solution)/shard_map/pallas_call | solution.py:332
  17.2 9.1 %shard_map.96.grid_ref = f32[1040,256]{1,0:T(8,128)S(1)} custom-call(f32[16,48,128]{2,1,0:T(8,128)S(1)} %get-tuple-element.13.merged, s32[8,128]{1,0:T(8,128)S(1)} %get-tuple-element.14.used_ref, f32[4,128,128]{2,1,0:T(8,128)S(1)} %get-tuple-element.15.phase_ref, f32[8,128]{1,0:T(8,128)S(1)} %get-tuple-element.16.kernel_ref), custom_call_target="tpu_custom_call" | custom-call | tf_op jit(solution)/shard_map/pallas_call | solution.py:461
  26.3 24.9 %shard_map.97 = (f32[64,64]{1,0:T(8,128)S(1)}, f32[4,128]{1,0:T(4,128)S(1)}) custom-call(f32[1040,256]{1,0:T(8,128)S(1)} %shard_map.96.grid_ref, bf16[2,256,256]{2,1,0:T(8,128)(2,1)S(1)} %get-tuple-element.17.matrix_ref, f32[7,2,128,128]{3,2,1,0:T(8,128)S(1)} %get-tuple-element.18.tw_ref, bf16[128,4096]{1,0:T(8,128)(2,1)S(1)} %get-tuple-element.19.onehot, ...), custom_call_target="tpu_custom_call" | custom-call | tf_op jit(solution)/shard_map/pallas_call | solution.py:682
  51.2 0.6 %copy.12 = f32[64,64]{1,0:T(8,128)} copy(f32[64,64]{1,0:T(8,128)S(1)} %get-tuple-element.26) | data formatting | bytes 32768
  51.8 0.6 %copy.13 = f32[512]{0:T(512)} copy(f32[512]{0:T(512)S(1)} %bitcast.4) | data formatting | bytes 4096

commit v5 on v4

--- a/solution.py
+++ b/solution.py
@@ -16,7 +16,6 @@
 TILES = 16
 BLOCKS = 128
 GROUP = 4
-CHUNK = 16
 F32 = jnp.float32
 BF16 = jnp.bfloat16
 I32 = jnp.int32
@@ -176,7 +175,7 @@
     barrier = pltpu.get_barrier_semaphore()
     for step in hops:
         pl.semaphore_signal(barrier, 1, device_id=device(h, step), device_id_type=MESH)
-    for step in (0,) + hops:
+    for step in (0, 2, -2):
         pl.semaphore_signal(barrier, 1, device_id=device(1 - h, step), device_id_type=MESH)
 
     upper = (iota((SLOTS, SLOTS), 0) < iota((SLOTS, SLOTS), 1)).astype(F32).astype(BF16)
@@ -190,7 +189,7 @@
         for index, part in enumerate(parts):
             packed[ch, 12 * index : 12 * index + 6] = part[:6, :128]
             packed[ch, 12 * index + 6 : 12 * index + 12] = part[:6, 128:]
-    pl.semaphore_wait(barrier, 9)
+    pl.semaphore_wait(barrier, 7)
 
     def direct(side, step, number):
         return pltpu.make_async_remote_copy(
@@ -217,10 +216,9 @@
     for step in (2, -2):
         copies.append(direct(1 - h, step, len(copies)))
         copies.append(direct(h, step, len(copies)))
+    copies.insert(2, direct(1 - h, 0, 4))
     for step in (1, -1):
-        copies.append(direct(1 - h, step, len(copies)))
         copies.append(direct(h, step, len(copies)))
-    copies.append(direct(1 - h, 0, len(copies)))
     for copy in copies:
         copy.start()
     own = pltpu.make_async_copy(packed.at[h], got.at[z, h], local)
@@ -246,6 +244,9 @@
         copy.start()
         relays.append(copy)
 
+    arrival(0, 1 - h).wait_recv()
+    pass_on(0, 1 - h, 1)
+    pass_on(0, 1 - h, -1)
     arrival(-2, h).wait_recv()
     pass_on(-2, h, 2)
     pass_on(-2, h, 1)
@@ -259,7 +260,6 @@
     for step in (1, -1):
         arrival(step, h).wait_recv()
         arrival(step, 1 - h).wait_recv()
-    arrival(0, 1 - h).wait_recv()
     for step in (3, -3, 4):
         arrival(step, h).wait_recv()
         arrival(step, 1 - h).wait_recv()
@@ -282,18 +282,16 @@
 
 
 def column_tables(z, kernel_ref, phase_ref):
-    l_row, lane = iota((128, 128), 0), iota((128, 128), 1)
-    l_val = (l_row & 63) + (l_row >> 6) * 512 + z * 64
-    phase_ref[0], phase_ref[1] = cis(l_val * lane, G)
-    zr, zi = cis(l_val, G)
+    l_row = iota((128, 128), 0)
+    zr, zi = cis((l_row & 63) + (l_row >> 6) * 512 + z * 64, G)
     kern = kernel_ref[...]
     pr = jnp.broadcast_to(kern[7:8], (128, 128))
     pi = jnp.zeros((128, 128), F32)
     for s in range(6, -1, -1):
         pr, pi = cmul(pr, pi, zr, zi)
         pr = pr + kern[s : s + 1]
-    phase_ref[2] = pr
-    phase_ref[3] = pi
+    phase_ref[0] = pr
+    phase_ref[1] = pi
 
 
 def row_tables(matrix_ref, twiddle_ref):
@@ -335,7 +333,7 @@
             jax.ShapeDtypeStruct((16, 48, 128), F32),
             jax.ShapeDtypeStruct((8, 128), F32),
             jax.ShapeDtypeStruct((8, 128), I32),
-            jax.ShapeDtypeStruct((4, 128, 128), F32),
+            jax.ShapeDtypeStruct((2, 128, 128), F32),
             jax.ShapeDtypeStruct((2, 256, 256), BF16),
             jax.ShapeDtypeStruct((7, 2, 128, 128), F32),
             jax.ShapeDtypeStruct((128, 4096), BF16),
@@ -355,9 +353,9 @@
             pltpu.VMEM((2, SLOTS), I32),
             pltpu.VMEM((2, SLOTS), I32),
             pltpu.VMEM((2, 2, SLOTS), I32),
-            pltpu.SemaphoreType.DMA((9,)),
+            pltpu.SemaphoreType.DMA((7,)),
             pltpu.SemaphoreType.DMA((8, 2)),
-            pltpu.SemaphoreType.DMA((6,)),
+            pltpu.SemaphoreType.DMA((8,)),
             pltpu.SemaphoreType.DMA,
             pltpu.SemaphoreType.DMA((8,)),
         ],
@@ -367,15 +365,21 @@
     )(*(pltpu.with_memory_space_constraint(x, pltpu.HBM) for x in args))
 
 
-def grid_kernel(merged, used_ref, phase_ref, kernel_ref, grid_ref, wbuf, rbuf, used, order, sem):
+def grid_kernel(merged, used_ref, taps_ref, kernel_ref, grid_ref, wbuf_a, rbuf_a, wbuf_b, rbuf_b, rows, used, order, sem):
     copy = pltpu.make_async_copy(used_ref, used, sem)
     copy.start()
     sub = iota((8, 128), 0)
-    ct_r, ct_i = cis(sub * iota((8, 128), 1), 8)
+    lane = iota((8, 128), 1)
+    _, z = places()
+    sd_r, sd_i = cis(sub * lane, G)
+    sc_r, sc_i = cis(sub * lane, 8)
+    gd_r, gd_i = cis((z * 64 + sub * 8) * lane, G)
+    gc_r, gc_i = cis((z * 64 + sub * 8) * lane, 8)
     grid_ref[...] = jnp.zeros_like(grid_ref)
-    for slot in range(2):
-        for i in range(GROUP):
-            rbuf[slot, i, 80:160, 128:256] = jnp.zeros((80, 128), BF16)
+    wbufs, rbufs = (wbuf_a, wbuf_b), (rbuf_a, rbuf_b)
+    for i in range(GROUP):
+        for ref in rbufs:
+            ref[i, 80:160, 128:256] = jnp.zeros((80, 128), BF16)
     copy.wait()
 
     def list_step(b, n):
@@ -383,7 +387,7 @@
         return n + jnp.where(used[0, b] > 0, 1, 0)
 
     total = lax.fori_loop(0, BLOCKS, list_step, 0, unroll=16)
-    for i in range(GROUP):
+    for i in range(2 * GROUP):
         order[total + i] = BLOCKS
 
     def build(bid, slot, i):
@@ -400,20 +404,26 @@
         index_u = field(4).astype(I32)
         index_v = field(5).astype(I32)
         w = field(2).astype(I32)
-        cr = take_lanes(ct_r, index_c)
-        ci = take_lanes(ct_i, index_c)
-        cr, ci = cmul(cr, ci, field(0) * keep, field(1) * keep)
-        for chunk in range(0, 16, CHUNK):
-            rows = [slice(8 * lg, 8 * lg + 8) for lg in range(chunk, chunk + CHUNK)]
-            phase = [(take_lanes(phase_ref[0, at], index_d), take_lanes(phase_ref[1, at], index_d)) for at in rows]
-            taps = [(take_lanes(phase_ref[2, at], index_v), take_lanes(phase_ref[3, at], index_v)) for at in rows]
-            done = [cmul(*cmul(*a, *b), cr, ci) for a, b in zip(phase, taps)]
-            for pair in range(CHUNK // 2):
-                for part in range(2):
-                    hi, lo = split2(jnp.concatenate([done[2 * pair][part], done[2 * pair + 1][part]], axis=0))
-                    start = part * 128 + 8 * chunk + 16 * pair
-                    wbuf[slot, i, start : start + 16, 0:128] = hi
-                    wbuf[slot, i, start : start + 16, 128:256] = lo
+        near = [take_lanes(t, index_d) for t in (gd_r, gd_i, sd_r, sd_i)]
+        wide = [take_lanes(t, index_c) for t in (gc_r, gc_i, sc_r, sc_i)]
+        group = cmul(*near[:2], *wide[:2])
+        inner = cmul(*cmul(*near[2:], *wide[2:]), field(0) * keep, field(1) * keep)
+        sign = (1 - 2 * (v & 1)).astype(F32)
+        rows[i, 0] = group[0]
+        rows[i, 1] = group[1]
+        for pair in range(4):
+            done = []
+            for g in (2 * pair, 2 * pair + 1):
+                ar, ai = cmul(jnp.broadcast_to(rows[i, 0, g : g + 1], (8, 128)), jnp.broadcast_to(rows[i, 1, g : g + 1], (8, 128)), *inner)
+                low, high = slice(8 * g, 8 * g + 8), slice(64 + 8 * g, 72 + 8 * g)
+                one = cmul(ar, ai, take_lanes(taps_ref[0, low], index_v), take_lanes(taps_ref[1, low], index_v))
+                two = cmul(ar * sign, ai * sign, take_lanes(taps_ref[0, high], index_v), take_lanes(taps_ref[1, high], index_v))
+                done.append(one + two)
+            for part, start in enumerate((0, 128, 64, 192)):
+                hi, lo = split2(jnp.concatenate([done[0][part], done[1][part]], axis=0))
+                at = slice(start + 16 * pair, start + 16 * pair + 16)
+                wbufs[slot][i, at, 0:128] = hi
+                wbufs[slot][i, at, 128:256] = lo
         taps = take_lanes(kernel_ref[...], index_u)
         turned = jnp.take_along_axis(taps, (sub - w) & 7, axis=0, mode="promise_in_bounds")
         high = turned.astype(BF16).astype(F32)
@@ -428,13 +438,13 @@
                 los.append(jnp.where(hit, low, zero))
             hi = jnp.concatenate(his, axis=0).astype(BF16)
             at = slice(16 * pair, 16 * pair + 16)
-            rbuf[slot, i, at, 0:128] = hi
-            rbuf[slot, i, at, 128:256] = hi
+            rbufs[slot][i, at, 0:128] = hi
+            rbufs[slot][i, at, 128:256] = hi
             at = slice(80 + 16 * pair, 80 + 16 * pair + 16)
-            rbuf[slot, i, at, 0:128] = jnp.concatenate(los, axis=0).astype(BF16)
+            rbufs[slot][i, at, 0:128] = jnp.concatenate(los, axis=0).astype(BF16)
 
     def place(bid, slot, i):
-        res = dot_nt(rbuf[slot, i], wbuf[slot, i])
+        res = dot_nt(rbufs[slot][i], wbufs[slot][i])
         start = pl.multiple_of(((bid >> 2) & 15) * 64, 64)
         grid_ref[pl.ds(start, 80), :] += res[:80] + res[80:]
 
@@ -445,16 +455,24 @@
         return bids
 
     def step(it, before):
-        slot = it & 1
+        first = tuple(order[2 * GROUP * it + i] for i in range(GROUP))
+        second = tuple(order[2 * GROUP * it + GROUP + i] for i in range(GROUP))
         for i in range(GROUP):
-            place(before[i], 1 - slot, i)
-        return fill(it, slot)
-
-    rounds = (total + GROUP - 1) // GROUP
-    last = lax.fori_loop(1, rounds, step, fill(0, 0))
-    slot = jnp.where(rounds > 0, (rounds - 1) & 1, 0)
+            place(before[i], 1, i)
+            build(first[i], 0, i)
+        for i in range(GROUP):
+            place(first[i], 0, i)
+            build(second[i], 1, i)
+        return second
+
+    rounds = (total + 2 * GROUP - 1) // (2 * GROUP)
     for i in range(GROUP):
-        place(last[i], slot, i)
+        rbufs[1][i, 0:80, 0:256] = jnp.zeros((80, 256), BF16)
+        rbufs[1][i, 80:160, 0:128] = jnp.zeros((80, 128), BF16)
+        wbufs[1][i] = jnp.zeros((256, 256), BF16)
+    last = lax.fori_loop(0, rounds, step, (jnp.int32(BLOCKS),) * GROUP)
+    for i in range(GROUP):
+        place(last[i], 1, i)
 
 
 def grid_call(merged, used, phase, kernel_t):
@@ -464,10 +482,13 @@
         in_specs=[VMEM_SPEC] * 4,
         out_specs=VMEM_SPEC,
         scratch_shapes=[
-            pltpu.VMEM((2, GROUP, 256, 256), BF16),
-            pltpu.VMEM((2, GROUP, 160, 256), BF16),
+            pltpu.VMEM((GROUP, 256, 256), BF16),
+            pltpu.VMEM((GROUP, 160, 256), BF16),
+            pltpu.VMEM((GROUP, 256, 256), BF16),
+            pltpu.VMEM((GROUP, 160, 256), BF16),
+            pltpu.VMEM((GROUP, 2, 8, 128), F32),
             pltpu.SMEM((8, 128), I32),
-            pltpu.SMEM((BLOCKS + GROUP,), I32),
+            pltpu.SMEM((BLOCKS + 2 * GROUP,), I32),
             pltpu.SemaphoreType.DMA,
         ],
         compiler_params=pltpu.CompilerParams(vmem_limit_bytes=LIMIT),

time: 52.3 us -> 49.8 us (0.952)
  Pallas kernels: 50.6 us -> 47.7 us
    pallas_call x1, Pallas kernels: 9.05 us -> 6.51 us  [grid_call(): pl.pallas_call(grid_kernel, out_shape=jax.ShapeDtypeStruct((1040, 256), F...]
    pallas_call x1, Pallas kernels: 24.9 us -> 24 us  [tail_call(): pl.pallas_call(tail_kernel, out_shape=(jax.ShapeDtypeStruct((64, 64), F32...]
    pallas_call x1, Pallas kernels: 16.6 us -> 17.1 us  [gather_call(): pl.pallas_call(gather_kernel, out_shape=(jax.ShapeDtypeStruct((16, 48, 12...]
where the time goes in v5:
time: 49.8 us; the launch traced here: 49.5 us
  Pallas kernels  47.7 us (96%)
  local copies, waits for them, and re-layouts  1.2 us (2%)
  between operations  0.66 us (1%)
    pallas_call x1, Pallas kernels, tail_call(): pl.pallas_call(tail_kernel, out_shape=(jax.ShapeDtypeStruct((64, 64), F32...  24 us
    pallas_call x1, Pallas kernels, gather_call(): pl.pallas_call(gather_kernel, out_shape=(jax.ShapeDtypeStruct((16, 48, 12...  17.1 us
    pallas_call x1, Pallas kernels, grid_call(): pl.pallas_call(grid_kernel, out_shape=jax.ShapeDtypeStruct((1040, 256), F...  6.51 us
    unnamed x2, local copies, waits for them, and re-layouts  1.2 us

profile of v5, /device:TPU:1, one launch (start us, length us, event | category | flops | bytes accessed | tf_op | source)
XLA Modules:
  0.0 49.5 jit_solution(1686871503636658659)
XLA Ops:
  0.6 17.1 %shard_map.95 = (f32[16,48,128]{2,1,0:T(8,128)S(1)}, f32[8,128]{1,0:T(8,128)S(1)}, s32[8,128]{1,0:T(8,128)S(1)}, f32[2,128,128]{2,1,0:T(8,128)S(1)}, bf16[2,256,...) custom-call(s32[1,2]{1,0:T(1,128)} %bitcast.7, ...), custom_call_target="tpu_custom_call" | custom-call | tf_op jit(solution)/shard_map/pallas_call | solution.py:330
  17.8 6.5 %shard_map.96.grid_ref = f32[1040,256]{1,0:T(8,128)S(1)} custom-call(f32[16,48,128]{2,1,0:T(8,128)S(1)} %get-tuple-element.13.merged, s32[8,128]{1,0:T(8,128)S(1)} %get-tuple-element.14.used_ref, f32[2,128,128]{2,1,0:T(8,128)S(1)} %get-tuple-element.15.taps_ref, f32[8,128]{1,0:T(8,128)S(1)} %get-tuple-element.16.kernel_ref), custom_call_target="tpu_custom_call" | custom-call | tf_op jit(solution)/shard_map/pallas_call | solution.py:479
  24.3 24.0 %shard_map.97 = (f32[64,64]{1,0:T(8,128)S(1)}, f32[4,128]{1,0:T(4,128)S(1)}) custom-call(f32[1040,256]{1,0:T(8,128)S(1)} %shard_map.96.grid_ref, bf16[2,256,256]{2,1,0:T(8,128)(2,1)S(1)} %get-tuple-element.17.matrix_ref, f32[7,2,128,128]{3,2,1,0:T(8,128)S(1)} %get-tuple-element.18.tw_ref, bf16[128,4096]{1,0:T(8,128)(2,1)S(1)} %get-tuple-element.19.onehot, ...), custom_call_target="tpu_custom_call" | custom-call | tf_op jit(solution)/shard_map/pallas_call | solution.py:703
  48.3 0.6 %copy.12 = f32[64,64]{1,0:T(8,128)} copy(f32[64,64]{1,0:T(8,128)S(1)} %get-tuple-element.26) | data formatting | bytes 32768
  48.9 0.6 %copy.13 = f32[512]{0:T(512)} copy(f32[512]{0:T(512)S(1)} %bitcast.4) | data formatting | bytes 4096

commit v6 on v5

--- a/solution.py
+++ b/solution.py
@@ -365,9 +365,7 @@
     )(*(pltpu.with_memory_space_constraint(x, pltpu.HBM) for x in args))
 
 
-def grid_kernel(merged, used_ref, taps_ref, kernel_ref, grid_ref, wbuf_a, rbuf_a, wbuf_b, rbuf_b, rows, used, order, sem):
-    copy = pltpu.make_async_copy(used_ref, used, sem)
-    copy.start()
+def gridder(merged, taps_ref, kernel_ref, grid_ref, wbufs, rbufs, rows):
     sub = iota((8, 128), 0)
     lane = iota((8, 128), 1)
     _, z = places()
@@ -376,23 +374,17 @@
     gd_r, gd_i = cis((z * 64 + sub * 8) * lane, G)
     gc_r, gc_i = cis((z * 64 + sub * 8) * lane, 8)
     grid_ref[...] = jnp.zeros_like(grid_ref)
-    wbufs, rbufs = (wbuf_a, wbuf_b), (rbuf_a, rbuf_b)
     for i in range(GROUP):
         for ref in rbufs:
             ref[i, 80:160, 128:256] = jnp.zeros((80, 128), BF16)
-    copy.wait()
-
-    def list_step(b, n):
-        order[n] = b
-        return n + jnp.where(used[0, b] > 0, 1, 0)
-
-    total = lax.fori_loop(0, BLOCKS, list_step, 0, unroll=16)
-    for i in range(2 * GROUP):
-        order[total + i] = BLOCKS
+    for i in range(GROUP):
+        rbufs[1][i, 0:80, 0:256] = jnp.zeros((80, 256), BF16)
+        rbufs[1][i, 80:160, 0:128] = jnp.zeros((80, 128), BF16)
+        wbufs[1][i] = jnp.zeros((256, 256), BF16)
 
     def build(bid, slot, i):
-        which = ((bid >> 6) & 1) * 8 + (bid & 7)
-        first = ((bid >> 3) & 7) * 6
+        which = lax.rem(lax.div(bid, 64), 2) * 8 + lax.rem(bid, 8)
+        first = lax.rem(lax.div(bid, 8), 8) * 6
         keep = jnp.where(bid < BLOCKS, 1.0, 0.0)
 
         def field(index):
@@ -445,14 +437,32 @@
 
     def place(bid, slot, i):
         res = dot_nt(rbufs[slot][i], wbufs[slot][i])
-        start = pl.multiple_of(((bid >> 2) & 15) * 64, 64)
+        start = pl.multiple_of(lax.rem(lax.div(bid, 4), 16) * 64, 64)
         grid_ref[pl.ds(start, 80), :] += res[:80] + res[80:]
 
-    def fill(it, slot):
-        bids = tuple(order[GROUP * it + i] for i in range(GROUP))
-        for i in range(GROUP):
-            build(bids[i], slot, i)
-        return bids
+    return build, place
+
+
+def grid_kernel(
+    merged, used_ref, taps_ref, kernel_ref, grid_ref, wbuf_a, rbuf_a, wbuf_b, rbuf_b, rows, used, order, sem
+):
+    copy = pltpu.make_async_copy(used_ref, used, sem)
+    copy.start()
+    build, place = gridder(
+        merged, taps_ref, kernel_ref, grid_ref, (wbuf_a, wbuf_b), (rbuf_a, rbuf_b), rows
+    )
+    copy.wait()
+
+    def list_step(four, n):
+        for extra in range(1, 4):
+            b = 4 * four + extra
+            order[n] = b
+            n = n + jnp.where(used[0, b] > 0, 1, 0)
+        return n
+
+    total = lax.fori_loop(0, BLOCKS // 4, list_step, 0, unroll=8)
+    for i in range(2 * GROUP):
+        order[total + i] = BLOCKS
 
     def step(it, before):
         first = tuple(order[2 * GROUP * it + i] for i in range(GROUP))
@@ -466,10 +476,6 @@
         return second
 
     rounds = (total + 2 * GROUP - 1) // (2 * GROUP)
-    for i in range(GROUP):
-        rbufs[1][i, 0:80, 0:256] = jnp.zeros((80, 256), BF16)
-        rbufs[1][i, 80:160, 0:128] = jnp.zeros((80, 128), BF16)
-        wbufs[1][i] = jnp.zeros((256, 256), BF16)
     last = lax.fori_loop(0, rounds, step, (jnp.int32(BLOCKS),) * GROUP)
     for i in range(GROUP):
         place(last[i], 1, i)
@@ -496,8 +502,8 @@
 
 
 def tail_kernel(
-    grid_ref, matrix_ref, tw_ref, onehot, hit_ref, counts, power_ref, spectrum_ref,
-    bh_ref, bl_ref, left, piece, partner, summed, landed, counts_in, counts_z, counts_plane,
+    grid_ref, merged, taps_ref, kernel_ref, matrix_ref, tw_ref, onehot, hit_ref, counts, power_ref, spectrum_ref,
+    first_ref, wbuf_a, rbuf_a, wbuf_b, rbuf_b, rows_ref, bh_ref, bl_ref, left, piece, partner, summed, landed, counts_in, counts_z, counts_plane,
     totals, totals_in, totals_z, totals_plane, sems,
 ):
     h, z = places()
@@ -526,13 +532,32 @@
             greet(chip((me_pair + k) % 16, to_core))
     greet(chip(me_pair, 1 - core))
 
+    build, place = gridder(
+        merged, taps_ref, kernel_ref, first_ref, (wbuf_a, wbuf_b), (rbuf_a, rbuf_b), rows_ref
+    )
+
+    def step(it, _):
+        for i in range(GROUP):
+            place(4 * ((2 * GROUP * it + 32 - GROUP + i) % 32), 1, i)
+            build(4 * (2 * GROUP * it + i), 0, i)
+        for i in range(GROUP):
+            place(4 * (2 * GROUP * it + i), 0, i)
+            build(4 * (2 * GROUP * it + GROUP + i), 1, i)
+        return 0
+
+    lax.fori_loop(0, 32 // (2 * GROUP), step, 0)
+    for i in range(GROUP):
+        place(4 * (32 - GROUP + i), 1, i)
+
     root = math.sqrt(0.5)
     slot_of = (0, 2, 4, 6, 1, 3, 5, 7)
     for rows in range(8):
         u = [
             (
-                grid_ref[128 * a + 16 * rows : 128 * a + 16 * rows + 16, 0:128],
-                grid_ref[128 * a + 16 * rows : 128 * a + 16 * rows + 16, 128:256],
+                grid_ref[128 * a + 16 * rows : 128 * a + 16 * rows + 16, 0:128]
+                + first_ref[128 * a + 16 * rows : 128 * a + 16 * rows + 16, 0:128],
+                grid_ref[128 * a + 16 * rows : 128 * a + 16 * rows + 16, 128:256]
+                + first_ref[128 * a + 16 * rows : 128 * a + 16 * rows + 16, 128:256],
             )
             for a in range(8)
         ]
@@ -698,14 +723,20 @@
         whole(totals_in, 15, 5).wait_send()
 
 
-def tail_call(grid, matrix, twiddle, onehot, hit, counts):
+def tail_call(*args):
     small = (4, 128)
     return pl.pallas_call(
         tail_kernel,
         out_shape=(jax.ShapeDtypeStruct((64, 64), F32), jax.ShapeDtypeStruct((4, 128), F32)),
-        in_specs=[VMEM_SPEC] * 6,
+        in_specs=[VMEM_SPEC] * 9,
         out_specs=(VMEM_SPEC,) * 2,
         scratch_shapes=[
+            pltpu.VMEM((1040, 256), F32),
+            pltpu.VMEM((GROUP, 256, 256), BF16),
+            pltpu.VMEM((GROUP, 160, 256), BF16),
+            pltpu.VMEM((GROUP, 256, 256), BF16),
+            pltpu.VMEM((GROUP, 160, 256), BF16),
+            pltpu.VMEM((GROUP, 2, 8, 128), F32),
             pltpu.VMEM((256, 1024), BF16),
             pltpu.VMEM((256, 1024), BF16),
             pltpu.VMEM((16, 4096), F32),
@@ -725,7 +756,27 @@
         compiler_params=pltpu.CompilerParams(
             collective_id=1, has_side_effects=True, vmem_limit_bytes=LIMIT
         ),
-    )(grid, matrix, twiddle, onehot, hit, counts)
+    )(*args)
+
+
+def store_kernel(power_ref, spectrum_ref, power_out, spectrum_out, sems):
+    first = pltpu.make_async_copy(power_ref, power_out, sems.at[0])
+    second = pltpu.make_async_copy(spectrum_ref, spectrum_out, sems.at[1])
+    first.start()
+    second.start()
+    first.wait()
+    second.wait()
+
+
+def store_call(power, spectrum):
+    return pl.pallas_call(
+        store_kernel,
+        out_shape=(jax.ShapeDtypeStruct((64, 64), F32), jax.ShapeDtypeStruct((4, 128), F32)),
+        in_specs=[VMEM_SPEC] * 2,
+        out_specs=(pl.BlockSpec(memory_space=pltpu.HBM),) * 2,
+        scratch_shapes=[pltpu.SemaphoreType.DMA((2,))],
+        compiler_params=pltpu.CompilerParams(vmem_limit_bytes=LIMIT),
+    )(power, spectrum)
 
 
 def per_device(visibility, tile_of, u_within, v_cell, kernel_index, kernel, live_count, bin_map):
@@ -740,7 +791,8 @@
         bin_map,
     )
     grid = grid_call(merged, used, phase, kernel_rows)
-    power, spectrum = tail_call(grid, matrix, twiddle, onehot, hit, counts)
+    power, spectrum = tail_call(grid, merged, phase, kernel_rows, matrix, twiddle, onehot, hit, counts)
+    power, spectrum = store_call(power, spectrum)
     return power, spectrum.reshape(NBINS)
 
 

time: 49.8 us -> 46.5 us (0.934)
  Pallas kernels: 47.7 us -> 45.8 us
  local copies, waits for them, and re-layouts: 1.2 us -> 0 us
    pallas_call x1, Pallas kernels: 6.51 us -> 3.76 us  [grid_call(): pl.pallas_call(grid_kernel, out_shape=jax.ShapeDtypeStruct((1040, 256), F...]
    unnamed x2 -> x0, local copies, waits for them, and re-layouts: 1.2 us -> none
    pallas_call x0 -> x1, Pallas kernels: none -> 0.64 us  [store_call(): pl.pallas_call(store_kernel, out_shape=(jax.ShapeDtypeStruct((64, 64), F3...]
where the time goes in v6:
time: 46.5 us; the launch traced here: 46.4 us
  Pallas kernels  45.8 us (98%)
  between operations  0.66 us (1%)
    pallas_call x1, Pallas kernels, tail_call(): pl.pallas_call(tail_kernel, out_shape=(jax.ShapeDtypeStruct((64, 64), F32...  24.2 us
    pallas_call x1, Pallas kernels, gather_call(): pl.pallas_call(gather_kernel, out_shape=(jax.ShapeDtypeStruct((16, 48, 12...  17.1 us
    pallas_call x1, Pallas kernels, grid_call(): pl.pallas_call(grid_kernel, out_shape=jax.ShapeDtypeStruct((1040, 256), F...  3.76 us

profile of v6, /device:TPU:1, one launch (start us, length us, event | category | flops | bytes accessed | tf_op | source)
XLA Modules:
  0.0 46.4 jit_solution(15519896742589494346)
XLA Ops:
  0.6 17.1 %shard_map.95 = (f32[16,48,128]{2,1,0:T(8,128)S(1)}, f32[8,128]{1,0:T(8,128)S(1)}, s32[8,128]{1,0:T(8,128)S(1)}, f32[2,128,128]{2,1,0:T(8,128)S(1)}, bf16[2,256,...) custom-call(s32[1,2]{1,0:T(1,128)} %bitcast.6, ...), custom_call_target="tpu_custom_call" | custom-call | tf_op jit(solution)/shard_map/pallas_call | solution.py:330
  17.8 3.8 %shard_map.96.grid_ref = f32[1040,256]{1,0:T(8,128)S(1)} custom-call(f32[16,48,128]{2,1,0:T(8,128)S(1)} %get-tuple-element.15.merged, s32[8,128]{1,0:T(8,128)S(1)} %get-tuple-element.16.used_ref, f32[2,128,128]{2,1,0:T(8,128)S(1)} %get-tuple-element.17.taps_ref, f32[8,128]{1,0:T(8,128)S(1)} %get-tuple-element.18.kernel_ref), custom_call_target="tpu_custom_call" | custom-call | tf_op jit(solution)/shard_map/pallas_call | solution.py:485
  21.5 24.2 %shard_map.97 = (f32[64,64]{1,0:T(8,128)S(1)}, f32[4,128]{1,0:T(4,128)S(1)}) custom-call(f32[1040,256]{1,0:T(8,128)S(1)} %shard_map.96.grid_ref, f32[16,48,128]{2,1,0:T(8,128)S(1)} %get-tuple-element.15.merged, f32[2,128,128]{2,1,0:T(8,128)S(1)} %get-tuple-element.17.taps_ref, f32[8,128]{1,0:T(8,128)S(1)} %get-tuple-element.18.kernel_ref, ...), custom_call_target="tpu_custom_call" | custom-call | tf_op jit(solution)/shard_map/pallas_call | solution.py:728
  45.8 0.6 %shard_map.98 = (f32[64,64]{1,0:T(8,128)}, f32[4,128]{1,0:T(4,128)}) custom-call(f32[64,64]{1,0:T(8,128)S(1)} %get-tuple-element.24.power_ref, f32[4,128]{1,0:T(4,128)S(1)} %get-tuple-element.25.spectrum_ref), custom_call_target="tpu_custom_call" | custom-call | tf_op jit(solution)/shard_map/pallas_call | solution.py:772

commit v7 on v6

--- a/solution.py
+++ b/solution.py
@@ -16,12 +16,17 @@
 TILES = 16
 BLOCKS = 128
 GROUP = 4
+TAIL = 24
 F32 = jnp.float32
 BF16 = jnp.bfloat16
 I32 = jnp.int32
 MESH = pl.DeviceIdType.MESH
 VMEM_SPEC = pl.BlockSpec(memory_space=pltpu.VMEM)
 LIMIT = 16 * 1024 * 1024
+STEPS = sorted(
+    ((down, right) for down in range(4) for right in range(4) if down or right),
+    key=lambda step: (-sum(min(part, 4 - part) for part in step), step),
+)
 NORM = 1.0 / (32 * 8192)
 
 
@@ -273,12 +278,12 @@
             for p in range(1, 8):
                 block = jnp.where(group == p, got[(p - i) % 8, half], block)
             out_ref[half * 8 + i] = block
-    nonzero = (out_ref[...].reshape(768, 128) != 0.0).astype(F32).astype(BF16)
-    found = dot_nt(jnp.ones((8, 128), F32).astype(BF16), nonzero).astype(BF16)
-    row, block = iota((768, 128), 0), iota((768, 128), 1)
-    first = ((block >> 6) * 8 + (block & 7)) * 48 + ((block >> 3) & 7) * 6
-    pick = ((row == first) | (row == first + 1)).astype(F32).astype(BF16)
-    used_ref[...] = dot_nn(found, pick).astype(I32)
+    marks = []
+    for index in range(16):
+        re, im = out_ref[index, pl.ds(0, 8, stride=6), :], out_ref[index, pl.ds(1, 8, stride=6), :]
+        marks.append(((re != 0.0) | (im != 0.0)).astype(F32))
+    marks = jnp.concatenate(marks, axis=0).astype(BF16)
+    used_ref[...] = dot_nt(jnp.ones((8, 128), F32).astype(BF16), marks).astype(I32)
 
 
 def column_tables(z, kernel_ref, phase_ref):
@@ -377,11 +382,6 @@
     for i in range(GROUP):
         for ref in rbufs:
             ref[i, 80:160, 128:256] = jnp.zeros((80, 128), BF16)
-    for i in range(GROUP):
-        rbufs[1][i, 0:80, 0:256] = jnp.zeros((80, 256), BF16)
-        rbufs[1][i, 80:160, 0:128] = jnp.zeros((80, 128), BF16)
-        wbufs[1][i] = jnp.zeros((256, 256), BF16)
-
     def build(bid, slot, i):
         which = lax.rem(lax.div(bid, 64), 2) * 8 + lax.rem(bid, 8)
         first = lax.rem(lax.div(bid, 8), 8) * 6
@@ -440,7 +440,15 @@
         start = pl.multiple_of(lax.rem(lax.div(bid, 4), 16) * 64, 64)
         grid_ref[pl.ds(start, 80), :] += res[:80] + res[80:]
 
-    return build, place
+    def open_round(first):
+        for i in range(GROUP):
+            build(4 * (first + i), 0, i)
+        for i in range(GROUP):
+            place(4 * (first + i), 0, i)
+            build(4 * (first + GROUP + i), 1, i)
+        return tuple(jnp.int32(4 * (first + GROUP + i)) for i in range(GROUP))
+
+    return build, place, open_round
 
 
 def grid_kernel(
@@ -448,19 +456,17 @@
 ):
     copy = pltpu.make_async_copy(used_ref, used, sem)
     copy.start()
-    build, place = gridder(
+    build, place, open_round = gridder(
         merged, taps_ref, kernel_ref, grid_ref, (wbuf_a, wbuf_b), (rbuf_a, rbuf_b), rows
     )
+    opened = open_round(TAIL)
     copy.wait()
-
-    def list_step(four, n):
-        for extra in range(1, 4):
-            b = 4 * four + extra
-            order[n] = b
-            n = n + jnp.where(used[0, b] > 0, 1, 0)
-        return n
-
-    total = lax.fori_loop(0, BLOCKS // 4, list_step, 0, unroll=8)
+    total = jnp.int32(0)
+    for half in range(2):
+        for i in (1, 2, 3, 5, 6, 7):
+            for g in range(8):
+                order[total] = half * 64 + g * 8 + i
+                total = total + jnp.where(used[0, half * 64 + i * 8 + g] > 0, 1, 0)
     for i in range(2 * GROUP):
         order[total + i] = BLOCKS
 
@@ -476,7 +482,7 @@
         return second
 
     rounds = (total + 2 * GROUP - 1) // (2 * GROUP)
-    last = lax.fori_loop(0, rounds, step, (jnp.int32(BLOCKS),) * GROUP)
+    last = lax.fori_loop(0, rounds, step, opened)
     for i in range(GROUP):
         place(last[i], 1, i)
 
@@ -512,6 +518,11 @@
     me = h * 16 + freq
     me_pair = h * 8 + quad
     far_first = (4, 3, 5, 2, 6, 1, 7)
+    row, spot = me_pair // 4, me_pair % 4
+
+    def neighbour(down, right):
+        return ((row + down) % 4) * 4 + (spot + right) % 4
+
 
     def chip(index, to_core):
         return {"freq": (index % 8) * 2 + to_core, "base": (index // 8) * 8 + z}
@@ -527,27 +538,28 @@
     for step in far_first:
         for to_core in range(2):
             greet(column(step, to_core))
-    for k in range(1, 16):
+    for step in STEPS:
         for to_core in range(2):
-            greet(chip((me_pair + k) % 16, to_core))
+            greet(chip(neighbour(*step), to_core))
     greet(chip(me_pair, 1 - core))
 
-    build, place = gridder(
+    build, place, open_round = gridder(
         merged, taps_ref, kernel_ref, first_ref, (wbuf_a, wbuf_b), (rbuf_a, rbuf_b), rows_ref
     )
+    open_round(0)
 
     def step(it, _):
         for i in range(GROUP):
-            place(4 * ((2 * GROUP * it + 32 - GROUP + i) % 32), 1, i)
+            place(4 * (2 * GROUP * it - GROUP + i), 1, i)
             build(4 * (2 * GROUP * it + i), 0, i)
         for i in range(GROUP):
             place(4 * (2 * GROUP * it + i), 0, i)
             build(4 * (2 * GROUP * it + GROUP + i), 1, i)
         return 0
 
-    lax.fori_loop(0, 32 // (2 * GROUP), step, 0)
+    lax.fori_loop(1, TAIL // (2 * GROUP), step, 0)
     for i in range(GROUP):
-        place(4 * (32 - GROUP + i), 1, i)
+        place(4 * (TAIL - GROUP + i), 1, i)
 
     root = math.sqrt(0.5)
     slot_of = (0, 2, 4, 6, 1, 3, 5, 7)
@@ -622,8 +634,8 @@
         def _():
             remote(buf, slots.at[me], number, chip(me_pair, 1)).start()
 
-        for k in range(1, 16):
-            remote(buf, slots.at[me], number, chip((me_pair + k) % 16, 1)).start()
+        for step in STEPS:
+            remote(buf, slots.at[me], number, chip(neighbour(*step), 1)).start()
 
     def plane_sum(buf, slots, result, number):
         slots[me] = buf[...]
@@ -669,8 +681,8 @@
         for side in range(2):
             for q in range(8):
                 summed[side * 8 + q, k0] = piece[core, k0, side, q] + partner[k0, side, q]
-    for k in range(1, 16):
-        peer = (me_pair + k) % 16
+    for step in STEPS:
+        peer = neighbour(*step)
         remote(summed.at[peer], landed.at[me_pair], 1, chip(peer, core)).start()
     landed[me_pair] = summed[me_pair]
 

time: 46.5 us -> 45.9 us (0.987)
  Pallas kernels: 45.8 us -> 45.3 us
    pallas_call x1, Pallas kernels: 24.2 us -> 23.2 us  [tail_call(): pl.pallas_call(tail_kernel, out_shape=(jax.ShapeDtypeStruct((64, 64), F32...]
    pallas_call x1, Pallas kernels: 3.76 us -> 4.53 us  [grid_call(): pl.pallas_call(grid_kernel, out_shape=jax.ShapeDtypeStruct((1040, 256), F...]
where the time goes in v7:
time: 45.9 us
  Pallas kernels  45.3 us (99%)
  between operations  0.66 us (1%)
    pallas_call x1, Pallas kernels, tail_call(): pl.pallas_call(tail_kernel, out_shape=(jax.ShapeDtypeStruct((64, 64), F32...  23.2 us
    pallas_call x1, Pallas kernels, gather_call(): pl.pallas_call(gather_kernel, out_shape=(jax.ShapeDtypeStruct((16, 48, 12...  16.9 us
    pallas_call x1, Pallas kernels, grid_call(): pl.pallas_call(grid_kernel, out_shape=jax.ShapeDtypeStruct((1040, 256), F...  4.53 us

profile of v7, /device:TPU:1, one launch (start us, length us, event | category | flops | bytes accessed | tf_op | source)
XLA Modules:
  0.0 45.9 jit_solution(9660343184698760656)
XLA Ops:
  0.6 16.9 %shard_map.95 = (f32[16,48,128]{2,1,0:T(8,128)S(1)}, f32[8,128]{1,0:T(8,128)S(1)}, s32[8,128]{1,0:T(8,128)S(1)}, f32[2,128,128]{2,1,0:T(8,128)S(1)}, bf16[2,256,...) custom-call(s32[1,2]{1,0:T(1,128)} %bitcast.6, ...), custom_call_target="tpu_custom_call" | custom-call | tf_op jit(solution)/shard_map/pallas_call | solution.py:335
  17.6 4.5 %shard_map.96.grid_ref = f32[1040,256]{1,0:T(8,128)S(1)} custom-call(f32[16,48,128]{2,1,0:T(8,128)S(1)} %get-tuple-element.15.merged, s32[8,128]{1,0:T(8,128)S(1)} %get-tuple-element.16.used_ref, f32[2,128,128]{2,1,0:T(8,128)S(1)} %get-tuple-element.17.taps_ref, f32[8,128]{1,0:T(8,128)S(1)} %get-tuple-element.18.kernel_ref), custom_call_target="tpu_custom_call" | custom-call | tf_op jit(solution)/shard_map/pallas_call | solution.py:491
  22.1 23.2 %shard_map.97 = (f32[64,64]{1,0:T(8,128)S(1)}, f32[4,128]{1,0:T(4,128)S(1)}) custom-call(f32[1040,256]{1,0:T(8,128)S(1)} %shard_map.96.grid_ref, f32[16,48,128]{2,1,0:T(8,128)S(1)} %get-tuple-element.15.merged, f32[2,128,128]{2,1,0:T(8,128)S(1)} %get-tuple-element.17.taps_ref, f32[8,128]{1,0:T(8,128)S(1)} %get-tuple-element.18.kernel_ref, ...), custom_call_target="tpu_custom_call" | custom-call | tf_op jit(solution)/shard_map/pallas_call | solution.py:740
  45.3 0.6 %shard_map.98 = (f32[64,64]{1,0:T(8,128)}, f32[4,128]{1,0:T(4,128)}) custom-call(f32[64,64]{1,0:T(8,128)S(1)} %get-tuple-element.24.power_ref, f32[4,128]{1,0:T(4,128)S(1)} %get-tuple-element.25.spectrum_ref), custom_call_target="tpu_custom_call" | custom-call | tf_op jit(solution)/shard_map/pallas_call | solution.py:784

commit v8 on v7

--- a/solution.py
+++ b/solution.py
@@ -172,16 +172,13 @@
     at = pl.multiple_of((freq // 2) * 128, 128)
     fetch = pltpu.make_async_copy(bins_ref.at[:, pl.ds(at, 128)], bins, fetched.at[7])
     fetch.start()
-    hops = (1, -1, 2, -2)
 
     def device(side, step):
         return {"base": side * 8 + (z + step + 8) % 8}
 
     barrier = pltpu.get_barrier_semaphore()
-    for step in hops:
-        pl.semaphore_signal(barrier, 1, device_id=device(h, step), device_id_type=MESH)
-    for step in (0, 2, -2):
-        pl.semaphore_signal(barrier, 1, device_id=device(1 - h, step), device_id_type=MESH)
+    for side, step in ((1 - h, 2), (1 - h, -2), (h, 2), (h, -2), (1 - h, 0), (h, 1), (h, -1)):
+        pl.semaphore_signal(barrier, 1, device_id=device(side, step), device_id_type=MESH)
 
     upper = (iota((SLOTS, SLOTS), 0) < iota((SLOTS, SLOTS), 1)).astype(F32).astype(BF16)
     for load in loads:
@@ -218,12 +215,8 @@
         )
 
     copies = []
-    for step in (2, -2):
-        copies.append(direct(1 - h, step, len(copies)))
-        copies.append(direct(h, step, len(copies)))
-    copies.insert(2, direct(1 - h, 0, 4))
-    for step in (1, -1):
-        copies.append(direct(h, step, len(copies)))
+    for side, step in ((1 - h, 2), (1 - h, -2), (h, 2), (h, -2), (1 - h, 0), (h, 1), (h, -1)):
+        copies.append(direct(side, step, len(copies)))
     for copy in copies:
         copy.start()
     own = pltpu.make_async_copy(packed.at[h], got.at[z, h], local)

time: 45.9 us -> 45.6 us (level)
    pallas_call x1, Pallas kernels: 4.53 us -> 3.89 us  [grid_call(): pl.pallas_call(grid_kernel, out_shape=jax.ShapeDtypeStruct((1040, 256), F...]
where the time goes in v8:
time: 45.6 us
  Pallas kernels  44.9 us (98%)
  between operations  0.66 us (1%)
    pallas_call x1, Pallas kernels, tail_call(): pl.pallas_call(tail_kernel, out_shape=(jax.ShapeDtypeStruct((64, 64), F32...  23.6 us
    pallas_call x1, Pallas kernels, gather_call(): pl.pallas_call(gather_kernel, out_shape=(jax.ShapeDtypeStruct((16, 48, 12...  16.8 us
    pallas_call x1, Pallas kernels, grid_call(): pl.pallas_call(grid_kernel, out_shape=jax.ShapeDtypeStruct((1040, 256), F...  3.89 us

profile of v8, /device:TPU:1, one launch (start us, length us, event | category | flops | bytes accessed | tf_op | source)
XLA Modules:
  0.0 45.6 jit_solution(2682442405447573737)
XLA Ops:
  0.6 16.8 %shard_map.95 = (f32[16,48,128]{2,1,0:T(8,128)S(1)}, f32[8,128]{1,0:T(8,128)S(1)}, s32[8,128]{1,0:T(8,128)S(1)}, f32[2,128,128]{2,1,0:T(8,128)S(1)}, bf16[2,256,...) custom-call(s32[1,2]{1,0:T(1,128)} %bitcast.6, ...), custom_call_target="tpu_custom_call" | custom-call | tf_op jit(solution)/shard_map/pallas_call | solution.py:328
  17.5 3.9 %shard_map.96.grid_ref = f32[1040,256]{1,0:T(8,128)S(1)} custom-call(f32[16,48,128]{2,1,0:T(8,128)S(1)} %get-tuple-element.15.merged, s32[8,128]{1,0:T(8,128)S(1)} %get-tuple-element.16.used_ref, f32[2,128,128]{2,1,0:T(8,128)S(1)} %get-tuple-element.17.taps_ref, f32[8,128]{1,0:T(8,128)S(1)} %get-tuple-element.18.kernel_ref), custom_call_target="tpu_custom_call" | custom-call | tf_op jit(solution)/shard_map/pallas_call | solution.py:484
  21.4 23.6 %shard_map.97 = (f32[64,64]{1,0:T(8,128)S(1)}, f32[4,128]{1,0:T(4,128)S(1)}) custom-call(f32[1040,256]{1,0:T(8,128)S(1)} %shard_map.96.grid_ref, f32[16,48,128]{2,1,0:T(8,128)S(1)} %get-tuple-element.15.merged, f32[2,128,128]{2,1,0:T(8,128)S(1)} %get-tuple-element.17.taps_ref, f32[8,128]{1,0:T(8,128)S(1)} %get-tuple-element.18.kernel_ref, ...), custom_call_target="tpu_custom_call" | custom-call | tf_op jit(solution)/shard_map/pallas_call | solution.py:733
  45.0 0.6 %shard_map.98 = (f32[64,64]{1,0:T(8,128)}, f32[4,128]{1,0:T(4,128)}) custom-call(f32[64,64]{1,0:T(8,128)S(1)} %get-tuple-element.24.power_ref, f32[4,128]{1,0:T(4,128)S(1)} %get-tuple-element.25.spectrum_ref), custom_call_target="tpu_custom_call" | custom-call | tf_op jit(solution)/shard_map/pallas_call | solution.py:777
